TPU v7x, 8 devices: a whole 2x2x1 slice. The times are simulated.
8 devices in a mesh: data: 1 (over z), tp: 8 (over y, x, core).
Axes of the slice: x: 2, y: 2, z: 1, core: 2. Of those that a mesh axis runs over, the one named last changes fastest.
Arguments:
- x_tokens: bfloat16 [4096, 1152], P(('data', 'tp'))
- ln_gamma: float32 [1152], replicated
- w_qkv: bfloat16 [1152, 16, 216], P(None, 'tp')
- w_out: bfloat16 [16, 72, 1152], P('tp')
- w_up: bfloat16 [1152, 4608], P(None, 'tp')
- w_down: bfloat16 [4608, 1152], P('tp')
Outputs:
- output: bfloat16 [4096, 1152], P(('data', 'tp'))
All inputs are finite; a program needn't handle non-finite values.
Results may differ from a plain program's by a relative error of at most 0.00218372.
Values are sent between devices in bfloat16 or wider.
A program may use at most 1 GiB of HBM per device.

v0:
```python
import math
import jax
import jax.numpy as jnp
from jax import lax
from jax.sharding import PartitionSpec as P

LN_EPS = 1e-6


def layer_norm(row_vals, ln_gain):
    row_mean = jnp.mean(row_vals, axis=-1, keepdims=True)
    centered = row_vals - row_mean
    row_var = jnp.mean(centered * centered, axis=-1, keepdims=True)
    return (centered * lax.rsqrt(row_var + LN_EPS) * ln_gain).astype(jnp.bfloat16)


def block_rows(row_count, head_count):
    return min(row_count, 2 ** int(math.log2(max(8, 4096 // head_count))))


def attend(query_rows, key_rows, value_rows):
    row_count, head_count, head_dim = query_rows.shape
    q_size = block_rows(row_count, head_count)
    attn_scale = head_dim ** -0.5

    def one_block(query_blk):
        scores = jnp.einsum("qhe,khe->hqk", query_blk, key_rows, preferred_element_type=jnp.float32) * attn_scale
        row_max = jnp.max(scores, axis=-1, keepdims=True)
        exp_scores = jnp.exp(scores - row_max)
        exp_sum = jnp.sum(exp_scores, axis=-1, keepdims=True)
        block_out = jnp.einsum("hqk,khe->hqe", exp_scores.astype(jnp.bfloat16), value_rows, preferred_element_type=jnp.float32)
        return (block_out / exp_sum).astype(jnp.bfloat16)

    return lax.map(one_block, query_rows.reshape(row_count // q_size, q_size, head_count, head_dim))


def solution(mesh):
    def local_block(x_loc, ln_gamma, w_qkv, w_out, w_up, w_down):
        model_dim = x_loc.shape[1]
        head_dim = w_qkv.shape[2] // 3
        residual = x_loc.astype(jnp.float32)
        normed = layer_norm(residual, ln_gamma)
        gathered = lax.all_gather(normed, "tp", axis=0, tiled=True)
        seq_len = gathered.shape[0]
        qkv_rows = jnp.einsum("sd,dhc->shc", gathered, w_qkv, preferred_element_type=jnp.float32).astype(jnp.bfloat16)
        head_out = attend(qkv_rows[:, :, :head_dim], qkv_rows[:, :, head_dim:2 * head_dim], qkv_rows[:, :, 2 * head_dim:])
        attn_part = jnp.einsum("nhqe,hed->nqd", head_out, w_out, preferred_element_type=jnp.float32).reshape(seq_len, model_dim)
        pre_act = jnp.dot(gathered, w_up, preferred_element_type=jnp.float32)
        hidden = jax.nn.gelu(pre_act, approximate=True).astype(jnp.bfloat16)
        part_sum = attn_part + jnp.dot(hidden, w_down, preferred_element_type=jnp.float32)
        reduced = lax.psum_scatter(part_sum, "tp", scatter_dimension=0, tiled=True)
        return (residual + reduced).astype(jnp.bfloat16)

    row_spec = P(("data", "tp"), None)
    return jax.shard_map(local_block, mesh=mesh, in_specs=(row_spec, P(None), P(None, "tp", None), P("tp", None, None), P(None, "tp"), P("tp", None)), out_specs=row_spec, check_vma=False)
```

profile of v0, /device:TPU:0, one launch (start us, length us, event | category | flops | bytes accessed | tf_op | source)
XLA Modules:
  0.0 381.4 jit_solution(10386123717602758132)
XLA Ops:
  6.5 0.0 copy-start
  6.5 0.0 copy-start.4
  6.5 0.0 all-gather.2.cloned.1.call-start
  6.5 1.6 convert_reduce_fusion
  8.2 0.0 copy-start.5
  8.2 1.8 fusion.36
  10.0 0.0 copy-done.1
  10.0 0.0 copy-done.4
  10.0 1.4 fusion.38
  11.5 0.0 all-gather.2.cloned.1.call-update
  11.5 0.0 reduce-scatter.2.cloned.1.call-start
  11.6 55.9 %all-gather.2.cloned.1.call-done = bf16[4096,1152]{1,0:T(8,128)(2,1)} async-done(((bf16[512,1152]{1,0:T(8,128)(2,1)}), bf16[4096,1152]{1,0:T(8,128)(2,1)}) %all-gather.2.cloned.1.call-update) | async-done | bytes 9437200 | tf_op jit(solution)/shard_map/all_gather | solution.py:43
  67.4 0.0 copy-done.5
  67.4 7.3 %fusion.49 = f32[4096,432]{0,1:S(1)} fusion(bf16[4096,1152]{1,0:T(8,128)(2,1)} %all-gather.2.cloned.1.call-done, bf16[1152,432]{0,1:T(8,128)(2,1)S(1)} %bitcast.42), kind=kOutput, calls=%fused_computation.48 | convolution fusion | flops 4076863488 | bytes 17510400
  74.8 0.5 convert_element_type.23
  75.3 1.4 fusion.46
  76.7 1.1 copy.11
  77.8 142.1 %while.10 = (s32[]{:T(128)}, bf16[2,2,2048,72]{2,3,1,0:T(8,128)(2,1)}, bf16[2,2048,2,72]{1,3,2,0:T(8,128)(2,1)}, bf16[4096,2,72]{0,2,1:T(8,128)(2,1)}, bf16[4096,2,72]{0,2,1:T(8,128)(2,1)S(1)}, /*index=5*/s32[]{:T(128)}) while((s32[]{:T(128)}, bf16[2,2,2048,72]{2,3,1,0:T(8,128)(2,1)}, bf16[2,2048,2,72]{1,3,2,0:T(8,128)(2,1)}, ...), condition=%wide.region_5.6_spmd, body=%wide.region_2.5_spmd.sunk | while | flops 4966637568 | bytes 204948560 | solution.py:34
  77.8 25.6 %multiply_reduce_fusion.2 = (f32[2,2048]{1,0:T(2,128)S(1)}, f32[2,2048,4096]{2,1,0:T(8,128)}) fusion(bf16[4096,2,72]{0,2,1:T(8,128)(2,1)} %get-tuple-element.103, bf16[2,2048,2,72]{1,3,2,0:T(8,128)(2,1)} %get-tuple-element.102, s32[]{:T(128)} %get-tuple-element.94), kind=kOutput, calls=%fused_computation.1.clone.1 | convolution fusion | flops 2449469440 | bytes 68895232 | tf_op jit(solution)/shard_map/while/body/eval_jaxpr/qhe,khe->hqk/dot_general | solution.py:27
  103.3 21.2 %fusion.66 = f32[2,2048]{1,0:T(2,128)S(1)} fusion(f32[2,2048,4096]{2,1,0:T(8,128)} %get-tuple-element.86, f32[2,2048]{1,0:T(2,128)S(1)} %get-tuple-element.87), kind=kLoop, calls=%fused_computation.2.clone.1 | loop fusion | flops 50327552 | bytes 67141632 | tf_op jit(solution)/shard_map/while/body/eval_jaxpr/reduce_sum | solution.py:30
  124.6 24.3 %fusion.67 = bf16[2,2,2048,72]{2,3,1,0:T(8,128)(2,1)} fusion(bf16[2,2,2048,72]{2,3,1,0:T(8,128)(2,1)} %get-tuple-element.95, s32[]{:T(128)} %get-tuple-element.94, bf16[4096,2,72]{0,2,1:T(8,128)(2,1)S(1)} %get-tuple-element.104, f32[2,2048,4096]{2,1,0:T(8,128)} %get-tuple-element.86, f32[2,2048]{1,0:T(2,128)S(1)} %get-tuple-element.87, ...), kind=kOutput, calls=%fused_computation.8.clone.1 | convolution fusion | flops 2466840576 | bytes 68911616 | tf_op jit(solution)/shard_map/while/body/eval_jaxpr/hqk,khe->hqe/dot_general | solution.py:31
  148.8 25.5 %multiply_reduce_fusion.2 = (f32[2,2048]{1,0:T(2,128)S(1)}, f32[2,2048,4096]{2,1,0:T(8,128)}) fusion(bf16[4096,2,72]{0,2,1:T(8,128)(2,1)} %get-tuple-element.103, bf16[2,2048,2,72]{1,3,2,0:T(8,128)(2,1)} %get-tuple-element.102, s32[]{:T(128)} %get-tuple-element.94), kind=kOutput, calls=%fused_computation.1.clone.1 | convolution fusion | flops 2449469440 | bytes 68895232 | tf_op jit(solution)/shard_map/while/body/eval_jaxpr/qhe,khe->hqk/dot_general | solution.py:27
  174.3 21.2 %fusion.66 = f32[2,2048]{1,0:T(2,128)S(1)} fusion(f32[2,2048,4096]{2,1,0:T(8,128)} %get-tuple-element.86, f32[2,2048]{1,0:T(2,128)S(1)} %get-tuple-element.87), kind=kLoop, calls=%fused_computation.2.clone.1 | loop fusion | flops 50327552 | bytes 67141632 | tf_op jit(solution)/shard_map/while/body/eval_jaxpr/reduce_sum | solution.py:30
  195.6 24.3 %fusion.67 = bf16[2,2,2048,72]{2,3,1,0:T(8,128)(2,1)} fusion(bf16[2,2,2048,72]{2,3,1,0:T(8,128)(2,1)} %get-tuple-element.95, s32[]{:T(128)} %get-tuple-element.94, bf16[4096,2,72]{0,2,1:T(8,128)(2,1)S(1)} %get-tuple-element.104, f32[2,2048,4096]{2,1,0:T(8,128)} %get-tuple-element.86, f32[2,2048]{1,0:T(2,128)S(1)} %get-tuple-element.87, ...), kind=kOutput, calls=%fused_computation.8.clone.1 | convolution fusion | flops 2466840576 | bytes 68911616 | tf_op jit(solution)/shard_map/while/body/eval_jaxpr/hqk,khe->hqe/dot_general | solution.py:31
  219.9 0.0 copy-done.3
  219.9 10.7 %fusion.40 = f32[2,2048,1152,1]{2,1,3,0:T(8,128)} fusion(bf16[2,2,2048,72]{2,3,1,0:T(8,128)(2,1)} %get-tuple-element.32, bf16[2,72,1152]{2,1,0:T(8,128)(2,1)S(1)} %copy-done.3), kind=kOutput, calls=%fused_computation.38 | convolution fusion | flops 1358954496 | bytes 20385792 | tf_op jit(solution)/shard_map/nhqe,hed->nqd/dot_general | solution.py:47
  230.6 0.0 copy-done
  230.6 23.9 %bitcast_add_fusion = f32[4096,1152]{1,0:T(8,128)} fusion(f32[2,2048,1152,1]{2,1,3,0:T(8,128)} %fusion.40, bf16[576,1152]{1,0:T(8,128)(2,1)S(1)} %copy-done, bf16[4096,1152]{1,0:T(8,128)(2,1)} %all-gather.2.cloned.1.call-done, bf16[1152,576]{0,1:T(8,128)(2,1)} %param.12), kind=kOutput, calls=%fused_computation.14 | convolution fusion | flops 10897588224 | bytes 49840128 | tf_op jit(solution)/shard_map/dot_general | solution.py:50
  254.5 0.0 reduce-scatter.2.cloned.1.call-update
  254.5 117.2 %reduce-scatter.2.cloned.1.call-done = f32[512,1152]{1,0:T(8,128)} async-done(((f32[4096,1152]{1,0:T(8,128)}), f32[512,1152]{1,0:T(8,128)}) %reduce-scatter.2.cloned.1.call-update) | async-done | bytes 2359312 | tf_op jit(solution)/shard_map/reduce_scatter | solution.py:51
  371.7 0.0 copy-done.2
  371.7 2.9 fusion.39
  (6 shorter events, 0.0 us)
Async XLA Ops:
  6.5 224.0 %copy-start = (bf16[576,1152]{1,0:T(8,128)(2,1)S(1)}, bf16[576,1152]{1,0:T(8,128)(2,1)}, u32[]{:S(2)}) copy-start(bf16[576,1152]{1,0:T(8,128)(2,1)} %param.13) | copy-start | bytes 3981316
  6.5 3.5 copy-start.1
  6.5 3.5 copy-start.4
  6.5 60.9 %all-gather.2.cloned.1.call-start = ((), (), s32[]{:S(2)}) async-start(), calls=%async_computation.1 | async-start | bytes 10616832 | tf_op jit(solution)/shard_map/all_gather | solution.py:43
  8.2 59.2 %copy-start.5 = (bf16[1152,2,216]{0,2,1:T(8,128)(2,1)S(1)}, bf16[1152,2,216]{0,2,1:T(8,128)(2,1)}, u32[]{:S(2)}) copy-start(bf16[1152,2,216]{0,2,1:T(8,128)(2,1)} %param.10) | copy-start | bytes 2985988
  11.5 360.2 %reduce-scatter.2.cloned.1.call-start = ((), (), s32[]{:S(2)}) async-start(), calls=%async_computation.2 | async-start | bytes 21233664 | tf_op jit(solution)/shard_map/reduce_scatter | solution.py:51
  77.8 142.1 %copy-start.3 = (bf16[2,72,1152]{2,1,0:T(8,128)(2,1)S(1)}, bf16[2,72,1152]{2,1,0:T(8,128)(2,1)}, u32[]{:S(2)}) copy-start(bf16[2,72,1152]{2,1,0:T(8,128)(2,1)} %param.11) | copy-start | bytes 995332
  254.5 117.2 %copy-start.2 = (bf16[512,1152]{1,0:T(8,128)(2,1)S(1)}, bf16[512,1152]{1,0:T(8,128)(2,1)}, u32[]{:S(2)}) copy-start(bf16[512,1152]{1,0:T(8,128)(2,1)} %param.8) | copy-start | bytes 3538948
Sparse Core Ops, SparseCore 0:
  11.6 55.7 all-gather.1
  254.6 117.0 reduce-scatter.1
where the time goes:
time: 382 us; the launch traced here: 381 us
  waiting for transfers between devices  173 us (45%)
  matrix products  142 us (37%)
  other arithmetic  50.8 us (13%)
  between operations  13.5 us (4%)
    reduce_scatter x1, waiting for transfers between devices, local_block(): reduced = lax.psum_scatter(part_sum, 'tp', scatter_dimension=0, tiled=True)  117 us
    all_gather x1, waiting for transfers between devices, local_block(): gathered = lax.all_gather(normed, 'tp', axis=0, tiled=True)  55.9 us
    dot_general x2, matrix products, one_block(): jnp.einsum('qhe,khe->hqk', query_blk, key_rows, preferred_element_type=jn...  51.1 us
    dot_general x2, matrix products, one_block(): jnp.einsum('hqk,khe->hqe', exp_scores.astype(jnp.bfloat16), value_rows, p...  48.5 us
    reduce_sum x2, other arithmetic, one_block(): exp_sum = jnp.sum(exp_scores, axis=-1, keepdims=True)  42.5 us
    dot_general x1, matrix products, local_block(): jnp.dot(hidden, w_down, preferred_element_type=jnp.float32)  23.9 us
    dot_general x1, matrix products, local_block(): jnp.einsum('nhqe,hed->nqd', head_out, w_out, preferred_element_type=jnp.f...  10.7 us
  transfers between devices with their start and end apart: 2, of which 2 were waited for; matrix products, arithmetic and copies ran while one was open for 0% of the time, Pallas kernels for 0%

commit v1 on v0

v1 whole, which is shorter than its diff:
```python
import math
import jax
import jax.numpy as jnp
from jax import lax
from jax.experimental import pallas as pl
from jax.experimental.pallas import tpu as pltpu
from jax.sharding import PartitionSpec as P

LN_EPS = 1e-6
LANES = 128
ROWS = 256
UNITS = 8
F32 = jnp.float32
BF16 = jnp.bfloat16


def gelu_tanh(v):
    return jax.nn.gelu(v, approximate=True)


def block_kernel(head_dim, head_rows, x_hbm, gamma_ref, wqkv_hbm, wout_hbm, w1_hbm, w2_hbm, y_ref,
                 x_ref, xg, wqkv, wout, w1, w2, q_all, k_all, v_all, part, recv, s_even, s_odd, m_even, m_odd, o_t,
                 load_sem, wsend, wrecv, gsend, grecv, kvsend, kvrecv, rsend, rrecv):
    me = lax.axis_index("tp")
    core = lax.rem(me, 2)
    chip_x = lax.rem(me // 2, 2)
    chip_y = me // 4
    sib = me + 1 - 2 * core
    x_nbr = me + 2 - 4 * chip_x
    y_nbr = me + 4 - 8 * chip_y

    def remote(src, dst, send, rcv, dev):
        return pltpu.make_async_remote_copy(src_ref=src, dst_ref=dst, send_sem=send, recv_sem=rcv,
                                            device_id={"tp": dev}, device_id_type=pl.DeviceIdType.MESH)

    own_out = wout.at[pl.ds(pl.multiple_of(core * 2 * head_rows, 2 * head_rows), 2 * head_rows)]

    loads = [
        pltpu.make_async_copy(x_hbm, x_ref, load_sem.at[0]),
        pltpu.make_async_copy(wqkv_hbm, wqkv.at[core], load_sem.at[1]),
        pltpu.make_async_copy(w1_hbm, w1.at[core], load_sem.at[2]),
        pltpu.make_async_copy(w2_hbm, w2.at[core], load_sem.at[3]),
        pltpu.make_async_copy(wout_hbm, own_out, load_sem.at[4]),
    ]
    for cp in loads:
        cp.start()

    barrier = pltpu.get_barrier_semaphore()
    for dev in (sib, x_nbr, y_nbr):
        pl.semaphore_signal(barrier, inc=1, device_id={"tp": dev}, device_id_type=pl.DeviceIdType.MESH)

    loads[0].wait()
    for half in (0, 1):
        rows = x_ref[pl.ds(half * ROWS, ROWS), :].astype(F32)
        mean = jnp.mean(rows, axis=-1, keepdims=True)
        cent = rows - mean
        var = jnp.mean(cent * cent, axis=-1, keepdims=True)
        xg[half] = (cent * lax.rsqrt(var + LN_EPS) * gamma_ref[...]).astype(BF16)

    pl.semaphore_wait(barrier, 3)

    def gather_copy(src, dst, idx, dev):
        return remote(xg.at[src], xg.at[dst], gsend.at[idx], grecv.at[idx], dev)

    g_copies = [
        gather_copy(0, 2, 0, y_nbr),
        gather_copy(1, 3, 1, x_nbr),
        gather_copy(0, 4, 2, x_nbr),
        gather_copy(1, 5, 3, y_nbr),
        gather_copy(2, 6, 4, x_nbr),
        gather_copy(3, 7, 5, y_nbr),
    ]
    for cp in g_copies[:4]:
        cp.start()
    w_copies = [
        remote(wqkv_hbm, wqkv.at[core], wsend.at[0], wrecv.at[0], sib),
        remote(w1_hbm, w1.at[core], wsend.at[1], wrecv.at[1], sib),
        remote(w2_hbm, w2.at[core], wsend.at[2], wrecv.at[2], sib),
        remote(wout_hbm, own_out, wsend.at[3], wrecv.at[3], sib),
    ]
    for cp in w_copies:
        cp.start()
    for cp in loads[1:]:
        cp.wait()
    for cp in w_copies:
        cp.wait_recv()

    def kv_copies(unit):
        return (
            remote(k_all.at[unit], k_all.at[UNITS + unit], kvsend.at[0, unit], kvrecv.at[0, unit], sib),
            remote(v_all.at[unit], v_all.at[UNITS + unit], kvsend.at[1, unit], kvrecv.at[1, unit], sib),
        )

    def project(unit, _):
        @pl.when(unit == 2)
        def _():
            g_copies[0].wait_recv()
            g_copies[4].start()
            g_copies[1].wait_recv()
            g_copies[5].start()

        @pl.when(unit == 4)
        def _():
            g_copies[2].wait_recv()
            g_copies[3].wait_recv()

        @pl.when(unit == 6)
        def _():
            g_copies[4].wait_recv()
            g_copies[5].wait_recv()

        rows = xg[unit]
        for s in (0, 1):
            qkv = jnp.dot(rows, wqkv[s], preferred_element_type=F32)
            for hh in (0, 1):
                h = 2 * s + hh
                base = hh * 3 * LANES
                q_all[unit, h] = qkv[:, base:base + LANES].astype(BF16)
                k_all[unit, h] = qkv[:, base + LANES:base + 2 * LANES].astype(BF16)
                v_t = jnp.transpose(qkv[:, base + 2 * LANES:base + 3 * LANES])
                v_all[unit, h] = v_t[:head_rows].astype(BF16)
        for cp in kv_copies(unit):
            cp.start()
        total = None
        for s in (0, 1):
            hidden = gelu_tanh(jnp.dot(rows, w1[s], preferred_element_type=F32)).astype(BF16)
            term = jnp.dot(hidden, w2[s], preferred_element_type=F32)
            total = term if total is None else total + term
        part[unit] = total
        return 0

    lax.fori_loop(0, UNITS, project, 0)

    def kv_wait(unit, _):
        for cp in kv_copies(unit):
            cp.wait()
        return 0

    lax.fori_loop(0, UNITS, kv_wait, 0)

    exp_scale = (head_dim ** -0.5) * math.log2(math.e)
    groups = ROWS // 8

    def score_chunk(c, unit, h, q, s_ref):
        s = lax.dot_general(k_all[c, h], q, (((1,), (1,)), ((), ())), preferred_element_type=F32)
        s_ref[pl.ds(c * ROWS, ROWS), :] = s
        return jnp.max(s.reshape(groups, 8, ROWS), axis=0)

    def scores(unit, h, s_ref, m_ref):
        q = q_all[unit, h]
        m = None
        for c in range(2 * UNITS):
            mc = score_chunk(c, unit, h, q, s_ref)
            m = mc if m is None else jnp.maximum(m, mc)
        m_ref[...] = m

    def finish(h, s_ref, m_ref, unit_n, h_n, s_next, m_next):
        q_n = q_all[unit_n, h_n]
        m = jnp.max(m_ref[...], axis=0, keepdims=True)
        acc = None
        total = None
        m_n = None
        for c in range(2 * UNITS):
            mc = score_chunk(c, unit_n, h_n, q_n, s_next)
            m_n = mc if m_n is None else jnp.maximum(m_n, mc)
            e = jnp.exp2((s_ref[pl.ds(c * ROWS, ROWS), :] - m) * exp_scale)
            tc = jnp.sum(e.reshape(groups, 8, ROWS), axis=0)
            total = tc if total is None else total + tc
            pv = jnp.dot(v_all[c, h], e.astype(BF16), preferred_element_type=F32)
            acc = pv if acc is None else acc + pv
        m_next[...] = m_n
        denom = jnp.sum(total, axis=0, keepdims=True)
        start = pl.multiple_of(h * head_rows, head_rows)
        o_t[pl.ds(start, head_rows), :] = (acc / denom).astype(BF16)

    def unit_of(i):
        return 2 * (3 - i // 2) + lax.rem(i, 2)

    def reduce_copy(idx, src, dev):
        return remote(part.at[src], recv.at[idx], rsend.at[idx], rrecv.at[idx], dev)

    r_copies = [
        reduce_copy(0, 6, x_nbr),
        reduce_copy(1, 7, y_nbr),
        reduce_copy(2, 4, x_nbr),
        reduce_copy(3, 5, y_nbr),
        reduce_copy(4, 2, y_nbr),
        reduce_copy(5, 3, x_nbr),
    ]

    scores(unit_of(0), 0, s_even, m_even)

    def attend(i, _):
        unit = unit_of(i)
        unit_next = unit_of(lax.rem(i + 1, UNITS))

        def pair(p, _):
            finish(2 * p, s_even, m_even, unit, 2 * p + 1, s_odd, m_odd)
            after = unit + p * (unit_next - unit)
            finish(2 * p + 1, s_odd, m_odd, after, 2 - 2 * p, s_even, m_even)
            return 0

        lax.fori_loop(0, 2, pair, 0)
        part[unit] += lax.dot_general(o_t[...], wout[...], (((0,), (0,)), ((), ())), preferred_element_type=F32)
        for step in range(6):
            @pl.when(i == step)
            def _():
                if step >= 4:
                    r_copies[step - 4].wait_recv()
                    part[step - 2] += recv[step - 4]
                r_copies[step].start()
        return 0

    lax.fori_loop(0, UNITS, attend, 0)

    for half, first, second in ((0, 2, 4), (1, 3, 5)):
        r_copies[first].wait_recv()
        r_copies[second].wait_recv()
        span = pl.ds(half * ROWS, ROWS)
        y_ref[span, :] = (x_ref[span, :].astype(F32) + part[half] + recv[first] + recv[second]).astype(BF16)
    for cp in g_copies + w_copies + r_copies:
        cp.wait_send()


def solution(mesh):
    def local_block(x_loc, ln_gamma, w_qkv, w_out, w_up, w_down):
        model_dim = x_loc.shape[1]
        heads = w_qkv.shape[1]
        head_dim = w_qkv.shape[2] // 3
        ff = w_up.shape[1]
        head_rows = -(-head_dim // 16) * 16
        wqkv = jnp.pad(w_qkv.reshape(model_dim, heads, 3, head_dim), ((0, 0), (0, 0), (0, 0), (0, LANES - head_dim)))
        wqkv = wqkv.reshape(model_dim, heads * 3 * LANES)
        wout = jnp.pad(w_out, ((0, 0), (0, head_rows - head_dim), (0, 0))).reshape(heads * head_rows, model_dim)
        any_spec = pl.BlockSpec(memory_space=pl.ANY)
        vmem_spec = pl.BlockSpec(memory_space=pltpu.VMEM)
        all_heads = 2 * heads
        keys = 2 * UNITS * ROWS
        dma = pltpu.SemaphoreType.DMA
        kern = lambda *refs: block_kernel(head_dim, head_rows, *refs)
        return pl.pallas_call(
            kern,
            out_shape=jax.ShapeDtypeStruct(x_loc.shape, BF16),
            in_specs=[any_spec, vmem_spec, any_spec, any_spec, any_spec, any_spec],
            out_specs=vmem_spec,
            scratch_shapes=[
                pltpu.VMEM(x_loc.shape, BF16),
                pltpu.VMEM((UNITS, ROWS, model_dim), BF16),
                pltpu.VMEM((2,) + wqkv.shape, BF16),
                pltpu.VMEM((all_heads * head_rows, model_dim), BF16),
                pltpu.VMEM((2, model_dim, ff), BF16),
                pltpu.VMEM((2, ff, model_dim), BF16),
                pltpu.VMEM((UNITS, all_heads, ROWS, LANES), BF16),
                pltpu.VMEM((2 * UNITS, all_heads, ROWS, LANES), BF16),
                pltpu.VMEM((2 * UNITS, all_heads, head_rows, ROWS), BF16),
                pltpu.VMEM((UNITS, ROWS, model_dim), F32),
                pltpu.VMEM((6, ROWS, model_dim), F32),
                pltpu.VMEM((keys, ROWS), F32),
                pltpu.VMEM((keys, ROWS), F32),
                pltpu.VMEM((8, ROWS), F32),
                pltpu.VMEM((8, ROWS), F32),
                pltpu.VMEM((all_heads * head_rows, ROWS), BF16),
                dma((5,)), dma((4,)), dma((4,)), dma((6,)), dma((6,)),
                dma((2, UNITS)), dma((2, UNITS)), dma((6,)), dma((6,)),
            ],
            compiler_params=pltpu.CompilerParams(collective_id=0, has_side_effects=True, vmem_limit_bytes=67043328),
            name="parallel_block",
        )(x_loc, ln_gamma.reshape(1, model_dim), wqkv, wout, w_up, w_down)

    row_spec = P(("data", "tp"), None)
    return jax.shard_map(local_block, mesh=mesh, in_specs=(row_spec, P(None), P(None, "tp", None), P("tp", None, None), P(None, "tp"), P("tp", None)), out_specs=row_spec, check_vma=False)
```

time: 382 us -> 151 us (0.40)
  waiting for transfers between devices: 173 us -> 0 us
  matrix products: 142 us -> 0 us
  Pallas kernels: 0 us -> 142 us
  other arithmetic: 50.8 us -> 0 us
  between operations: 13.5 us -> 0.03 us
  local copies, waits for them, and re-layouts: 2.51 us -> 9.09 us
    pallas_call x0 -> x1, Pallas kernels: none -> 142 us  [local_block(): pl.pallas_call(kern, out_shape=jax.ShapeDtypeStruct(x_loc.shape, BF16), i...]
    dot_general x6 -> x0, matrix products: 134 us -> none  [the longest x2 51.1 us: one_block(): jnp.einsum('qhe,khe->hqk', query_blk, key_rows, preferred_element_type=jn...]
    reduce_scatter x1 -> x0, waiting for transfers between devices: 117 us -> none  [local_block(): reduced = lax.psum_scatter(part_sum, 'tp', scatter_dimension=0, tiled=True)]
    all_gather x1 -> x0, waiting for transfers between devices: 55.9 us -> none  [local_block(): gathered = lax.all_gather(normed, 'tp', axis=0, tiled=True)]
    reduce_sum x4 -> x0, other arithmetic: 45.9 us -> none  [the longest x2 42.5 us: one_block(): exp_sum = jnp.sum(exp_scores, axis=-1, keepdims=True)]
    unnamed x1 -> x0, matrix products: 7.32 us -> none
    convert_element_type x3 -> x0, other arithmetic: 4.82 us -> none  [the longest x1 2.88 us: local_block(): return (residual + reduced).astype(jnp.bfloat16)]
    unnamed x12 -> x8, local copies, waits for them, and re-layouts: 0.02 us -> 4.03 us
  transfers between devices with their start and end apart: 2 -> 0, of which waited for: 2 -> 0; matrix products, arithmetic and copies ran while one was open for 0% -> 0% of each run, Pallas kernels for 0% -> 0%
where the time goes in v1:
time: 151 us
  Pallas kernels  142 us (94%)
  local copies, waits for them, and re-layouts  9.09 us (6%)
    pallas_call x1, Pallas kernels, local_block(): pl.pallas_call(kern, out_shape=jax.ShapeDtypeStruct(x_loc.shape, BF16), i...  142 us
    unnamed x8, local copies, waits for them, and re-layouts  4.03 us

profile of v1, /device:TPU:0, one launch (start us, length us, event | category | flops | bytes accessed | tf_op | source)
XLA Modules:
  0.0 151.2 jit_solution(5187313224709170924)
XLA Ops:
  0.0 1.4 pad.8
  1.4 0.0 copy-start
  1.4 2.3 %copy.9.refs_2_ = bf16[1152,768]{1,0:T(8,128)(2,1)} copy(bf16[1152,768]{0,1:T(8,128)(2,1)S(1)} %bitcast.3) | data formatting | bytes 3538944 | tf_op jit(solution)/shard_map/reshape | solution.py:233
  3.7 0.0 copy-done
  3.7 0.0 copy-start.1
  3.7 0.0 copy-start.2
  3.7 1.6 %copy.10.refs_4_ = bf16[1152,576]{1,0:T(8,128)(2,1)} copy(bf16[1152,576]{0,1:T(8,128)(2,1)S(1)} %copy-done) | data formatting | bytes 2654208 | tf_op args[4]
  5.4 0.0 copy-done.1
  5.4 0.8 pad.9
  6.1 0.0 copy-done.2
  6.1 0.6 reshape.12.refs_1_
  6.7 142.1 %parallel_block.1 = bf16[512,1152]{1,0:T(8,128)(2,1)} custom-call(bf16[512,1152]{1,0:T(8,128)(2,1)} %refs_0_.1, f32[1,1152]{1,0:T(1,128)} %reshape.12.refs_1_, bf16[1152,768]{1,0:T(8,128)(2,1)} %copy.9.refs_2_, bf16[160,1152]{1,0:T(8,128)(2,1)} %bitcast.4, bf16[1152,576]{1,0:T(8,128)(2,1)} %copy.10.refs_4_, bf16[576,1152]{1,0:T(8,128)(2,1)} %refs_5_.1), custom_call_target="tpu_custom_call" | custom-call | tf_op jit(solution)/shard_map/parallel_block/pallas_call | solution.py:241
  148.8 2.4 %copy.12 = bf16[512,1152]{1,0:T(8,128)(2,1)} copy(bf16[512,1152]{1,0:T(8,128)(2,1)} %parallel_block.1) | data formatting | bytes 2359296
Async XLA Ops:
  1.4 2.3 %copy-start = (bf16[1152,576]{0,1:T(8,128)(2,1)S(1)}, bf16[1152,576]{0,1:T(8,128)(2,1)}, u32[]{:S(2)}) copy-start(bf16[1152,576]{0,1:T(8,128)(2,1)} %param.10) | copy-start | bytes 3981316
  3.7 1.7 %copy-start.1 = (bf16[2,72,1152]{2,1,0:T(8,128)(2,1)S(1)}, bf16[2,72,1152]{2,1,0:T(8,128)(2,1)}, u32[]{:S(2)}) copy-start(bf16[2,72,1152]{2,1,0:T(8,128)(2,1)} %param.9) | copy-start | bytes 995332
  3.7 2.4 %copy-start.2 = (f32[1152]{0:T(1024)S(1)}, f32[1152]{0:T(1024)}, u32[]{:S(2)}) copy-start(f32[1152]{0:T(1024)} %param.7) | copy-start | bytes 13828

commit v2 on v0

v2 whole, which is shorter than its diff:
```python
import functools
import math
import jax
import jax.numpy as jnp
from jax import lax
from jax.experimental import pallas as pl
from jax.experimental.pallas import tpu as pltpu
from jax.sharding import PartitionSpec as P

LN_EPS = 1e-6
LANES = 128
ROWS = 256
UNITS = 8
CHUNKS = 2 * UNITS
HEADS = 4
F32 = jnp.float32
BF16 = jnp.bfloat16
ROW_MAJOR = (((1,), (0,)), ((), ()))
BY_ROWS = (((1,), (1,)), ((), ()))
BY_COLS = (((0,), (0,)), ((), ()))


def dot(a, b, dims=ROW_MAJOR):
    return lax.dot_general(a, b, dims, preferred_element_type=F32)


def gelu_tanh(v):
    return jax.nn.gelu(v, approximate=True)


def block_kernel(head_dim, head_rows, x_hbm, gamma_ref, wqkv_hbm, wout_hbm, w1_hbm, w2_hbm, y_ref,
                 xg, xn, wqv, wk, wout, w1, w2, q_all, k_all, v_all, part, recv, s_even, s_odd, m_even, m_odd, o_t,
                 acc_st, m_st, l_st,
                 load_sem, wsend, wrecv, gsend, grecv, kvsend, kvrecv, rsend, rrecv):
    me = lax.axis_index("tp")
    core = lax.rem(me, 2)
    chip_x = lax.rem(me // 2, 2)
    chip_y = me // 4
    sib = me + 1 - 2 * core
    x_nbr = me + 2 - 4 * chip_x
    y_nbr = me + 4 - 8 * chip_y
    mesh_id = pl.DeviceIdType.MESH

    def remote(src, dst, send, rcv, dev):
        return pltpu.make_async_remote_copy(src_ref=src, dst_ref=dst, send_sem=send, recv_sem=rcv,
                                            device_id={"tp": dev}, device_id_type=mesh_id)

    wqv[:, :, head_rows - 16:, :] = jnp.zeros((2, HEADS, 16, wqv.shape[3]), BF16)
    wk[:, LANES - 64:, :] = jnp.zeros((HEADS, 64, wk.shape[2]), BF16)
    wout[:, head_rows - 16:, :] = jnp.zeros((HEADS, 16, wout.shape[2]), BF16)

    barrier = pltpu.get_barrier_semaphore()
    for dev in (sib, x_nbr, y_nbr):
        pl.semaphore_signal(barrier, inc=1, device_id={"tp": dev}, device_id_type=mesh_id)

    pairs = []
    for hh in (0, 1):
        h = 2 * core + hh
        real = pl.ds(0, head_dim)
        pairs += [
            (wqkv_hbm.at[hh, pl.ds(0, head_dim)], wqv.at[0, h, real]),
            (wqkv_hbm.at[hh, pl.ds(head_dim, head_dim)], wk.at[h, real]),
            (wqkv_hbm.at[hh, pl.ds(2 * head_dim, head_dim)], wqv.at[1, h, real]),
            (wout_hbm.at[hh], wout.at[h, real]),
        ]
    pairs += [(w1_hbm, w1.at[core]), (w2_hbm, w2.at[core])]
    loads = [pltpu.make_async_copy(x_hbm.at[pl.ds(half * ROWS, ROWS)], xg.at[half], load_sem.at[half]) for half in (0, 1)]
    loads += [pltpu.make_async_copy(src, dst, load_sem.at[2 + n]) for n, (src, dst) in enumerate(pairs)]
    for cp in loads:
        cp.start()

    pl.semaphore_wait(barrier, 3)

    def gather_copy(src, dst, idx, dev):
        return remote(src, xg.at[dst], gsend.at[idx], grecv.at[idx], dev)

    half_1, half_2 = x_hbm.at[pl.ds(0, ROWS)], x_hbm.at[pl.ds(ROWS, ROWS)]
    g_copies = [
        gather_copy(half_1, 2, 0, y_nbr),
        gather_copy(half_2, 3, 1, x_nbr),
        gather_copy(half_1, 4, 2, x_nbr),
        gather_copy(half_2, 5, 3, y_nbr),
        gather_copy(xg.at[2], 6, 4, x_nbr),
        gather_copy(xg.at[3], 7, 5, y_nbr),
    ]
    for cp in g_copies[:4]:
        cp.start()
    w_copies = [remote(src, dst, wsend.at[n], wrecv.at[n], sib) for n, (src, dst) in enumerate(pairs)]
    for cp in w_copies:
        cp.start()

    zero_rows = LANES - head_rows

    def clear(unit, _):
        q_all[unit, :, head_rows:, :] = jnp.zeros((HEADS, zero_rows, ROWS), BF16)
        return 0

    lax.fori_loop(0, UNITS, clear, 0)

    def kv_copies(unit):
        return (
            remote(k_all.at[unit], k_all.at[UNITS + unit], kvsend.at[0, unit], kvrecv.at[0, unit], sib),
            remote(v_all.at[unit], v_all.at[UNITS + unit], kvsend.at[1, unit], kvrecv.at[1, unit], sib),
        )

    def project(unit, _):
        rows = xg[unit].astype(F32)
        mean = jnp.mean(rows, axis=-1, keepdims=True)
        cent = rows - mean
        var = jnp.mean(cent * cent, axis=-1, keepdims=True)
        normed = (cent * lax.rsqrt(var + LN_EPS) * gamma_ref[...]).astype(BF16)
        xn[unit] = normed
        keys = dot(normed, wk[...].reshape(HEADS * LANES, -1), BY_ROWS)
        qv = dot(wqv[...].reshape(2 * HEADS * head_rows, -1), normed, BY_ROWS).astype(BF16)
        for h in range(HEADS):
            k_all[unit, h] = keys[:, h * LANES:(h + 1) * LANES].astype(BF16)
            q_all[unit, h, :head_rows] = qv[h * head_rows:(h + 1) * head_rows]
            v_all[unit, h] = qv[(HEADS + h) * head_rows:(HEADS + h + 1) * head_rows]
        for cp in kv_copies(unit):
            cp.start()
        return 0

    def mlp(unit, _):
        rows = xn[unit]
        total = None
        for s in (0, 1):
            hidden = gelu_tanh(dot(rows, w1[s], BY_ROWS)).astype(BF16)
            term = dot(hidden, w2[s])
            total = term if total is None else total + term
        part[unit] = total
        return 0

    def kv_wait(unit, _):
        for cp in kv_copies(unit):
            cp.wait()
        return 0

    exp_scale = (head_dim ** -0.5) * math.log2(math.e)
    groups = ROWS // 8

    def score_chunk(n, c, h, q, s_ref):
        s = dot(k_all[c, h], q)
        s_ref[pl.ds(n * ROWS, ROWS), :] = s
        return jnp.max(s.reshape(groups, 8, ROWS), axis=0)

    def finish(chunks, h, s_ref, m_ref, unit_n, h_n, s_next, m_next):
        q_n = q_all[unit_n, h_n]
        m = jnp.max(m_ref[...], axis=0, keepdims=True)
        acc = None
        total = None
        m_n = None
        for n, c in enumerate(chunks):
            mc = score_chunk(n, c, h_n, q_n, s_next)
            m_n = mc if m_n is None else jnp.maximum(m_n, mc)
            e = jnp.exp2((s_ref[pl.ds(n * ROWS, ROWS), :] - m) * exp_scale)
            tc = jnp.sum(e.reshape(groups, 8, ROWS), axis=0)
            total = tc if total is None else total + tc
            pv = dot(v_all[c, h], e.astype(BF16))
            acc = pv if acc is None else acc + pv
        m_next[...] = m_n
        return m, jnp.sum(total, axis=0, keepdims=True), acc

    def attend(count, unit_of, chunks, emit, after):
        q = q_all[unit_of(0), 0]
        m = None
        for n, c in enumerate(chunks):
            mc = score_chunk(n, c, 0, q, s_even)
            m = mc if m is None else jnp.maximum(m, mc)
        m_even[...] = m

        def one(i, _):
            unit = unit_of(i)
            unit_next = unit_of(lax.rem(i + 1, count))

            def pair(p, _):
                emit(i, 2 * p, *finish(chunks, 2 * p, s_even, m_even, unit, 2 * p + 1, s_odd, m_odd))
                follow = unit + p * (unit_next - unit)
                emit(i, 2 * p + 1, *finish(chunks, 2 * p + 1, s_odd, m_odd, follow, 2 - 2 * p, s_even, m_even))
                return 0

            lax.fori_loop(0, 2, pair, 0)
            after(i, unit)
            return 0

        lax.fori_loop(0, count, one, 0)

    def emit_state(i, h, m, total, acc):
        m_st[i, h] = jnp.broadcast_to(m, m_st.shape[2:])
        l_st[i, h] = jnp.broadcast_to(total, l_st.shape[2:])
        acc_st[i, h] = acc

    def emit_merged(i, h, m, total, acc):
        m_old = m_st[i, h][:1]
        top = jnp.maximum(m, m_old)
        a_new = jnp.exp2((m - top) * exp_scale)
        a_old = jnp.exp2((m_old - top) * exp_scale)
        denom = total * a_new + l_st[i, h][:1] * a_old
        o_t[h] = ((acc * a_new + acc_st[i, h] * a_old) / denom).astype(BF16)

    def emit_out(i, h, m, total, acc):
        o_t[h] = (acc / total).astype(BF16)

    def add_heads(unit):
        part[unit] += dot(o_t[...].reshape(HEADS * head_rows, ROWS), wout[...].reshape(HEADS * head_rows, -1), BY_COLS)

    def reduce_copy(idx, src, dev):
        return remote(part.at[src], recv.at[idx], rsend.at[idx], rrecv.at[idx], dev)

    r_copies = [
        reduce_copy(0, 2, y_nbr),
        reduce_copy(1, 3, x_nbr),
        reduce_copy(2, 6, y_nbr),
        reduce_copy(3, 7, x_nbr),
        reduce_copy(4, 4, x_nbr),
        reduce_copy(5, 5, y_nbr),
    ]

    for cp in loads[2:]:
        cp.wait()
    for cp in w_copies:
        cp.wait_recv()
    for cp in loads[:2]:
        cp.wait()
    lax.fori_loop(0, 2, project, 0)
    lax.fori_loop(0, 2, mlp, 0)
    g_copies[0].wait_recv()
    g_copies[4].start()
    g_copies[1].wait_recv()
    g_copies[5].start()
    lax.fori_loop(2, 4, project, 0)
    lax.fori_loop(2, 4, mlp, 0)
    g_copies[2].wait_recv()
    g_copies[3].wait_recv()
    lax.fori_loop(4, 6, project, 0)
    lax.fori_loop(0, 6, kv_wait, 0)
    early = [c for c in range(CHUNKS) if c % UNITS < 6]
    late = [c for c in range(CHUNKS) if c % UNITS >= 6]
    attend(2, lambda i: 2 + i, early, emit_state, lambda i, unit: None)
    g_copies[4].wait_recv()
    g_copies[5].wait_recv()
    lax.fori_loop(6, 8, project, 0)
    lax.fori_loop(6, 8, kv_wait, 0)

    def after_first(i, unit):
        add_heads(unit)
        for step in (0, 1):
            @pl.when(i == step)
            def _():
                r_copies[step].start()

    attend(2, lambda i: 2 + i, late, emit_merged, after_first)
    lax.fori_loop(4, 8, mlp, 0)

    def later_unit(i):
        p = i // 2
        return 2 * (3 - p - p // 2) + lax.rem(i, 2)

    def after_later(i, unit):
        add_heads(unit)
        for step in range(4):
            @pl.when(i == step)
            def _():
                if step >= 2:
                    r_copies[step].wait_recv()
                    part[step + 2] += recv[step]
                r_copies[step + 2].start()

    attend(6, later_unit, list(range(CHUNKS)), emit_out, after_later)

    for half, first, second in ((0, 0, 4), (1, 1, 5)):
        r_copies[first].wait_recv()
        r_copies[second].wait_recv()
        span = pl.ds(half * ROWS, ROWS)
        y_ref[span, :] = (xg[half].astype(F32) + part[half] + recv[first] + recv[second]).astype(BF16)
    for cp in g_copies + w_copies + r_copies:
        cp.wait_send()


def solution(mesh):
    def local_block(x_loc, ln_gamma, w_qkv, w_out, w_up, w_down):
        model_dim = x_loc.shape[1]
        head_dim = w_qkv.shape[2] // 3
        ff = w_up.shape[1]
        head_rows = -(-head_dim // 16) * 16
        hbm = pl.BlockSpec(memory_space=pltpu.HBM)
        vmem = pl.BlockSpec(memory_space=pltpu.VMEM)
        dma = pltpu.SemaphoreType.DMA
        return pl.pallas_call(
            functools.partial(block_kernel, head_dim, head_rows),
            out_shape=jax.ShapeDtypeStruct(x_loc.shape, BF16),
            in_specs=[hbm, vmem, hbm, hbm, hbm, hbm],
            out_specs=vmem,
            scratch_shapes=[
                pltpu.VMEM((UNITS, ROWS, model_dim), BF16),
                pltpu.VMEM((UNITS, ROWS, model_dim), BF16),
                pltpu.VMEM((2, HEADS, head_rows, model_dim), BF16),
                pltpu.VMEM((HEADS, LANES, model_dim), BF16),
                pltpu.VMEM((HEADS, head_rows, model_dim), BF16),
                pltpu.VMEM((2, ff, model_dim), BF16),
                pltpu.VMEM((2, ff, model_dim), BF16),
                pltpu.VMEM((UNITS, HEADS, LANES, ROWS), BF16),
                pltpu.VMEM((CHUNKS, HEADS, ROWS, LANES), BF16),
                pltpu.VMEM((CHUNKS, HEADS, head_rows, ROWS), BF16),
                pltpu.VMEM((UNITS, ROWS, model_dim), F32),
                pltpu.VMEM((6, ROWS, model_dim), F32),
                pltpu.VMEM((CHUNKS * ROWS, ROWS), F32),
                pltpu.VMEM((CHUNKS * ROWS, ROWS), F32),
                pltpu.VMEM((8, ROWS), F32),
                pltpu.VMEM((8, ROWS), F32),
                pltpu.VMEM((HEADS, head_rows, ROWS), BF16),
                pltpu.VMEM((2, HEADS, head_rows, ROWS), F32),
                pltpu.VMEM((2, HEADS, 8, ROWS), F32),
                pltpu.VMEM((2, HEADS, 8, ROWS), F32),
                dma((12,)), dma((10,)), dma((10,)), dma((6,)), dma((6,)),
                dma((2, UNITS)), dma((2, UNITS)), dma((6,)), dma((6,)),
            ],
            compiler_params=pltpu.CompilerParams(collective_id=0, has_side_effects=True, vmem_limit_bytes=67043328),
            name="parallel_block",
        )(x_loc, ln_gamma.reshape(1, model_dim), w_qkv.transpose(1, 2, 0), w_out, w_up.T, w_down)

    row_spec = P(("data", "tp"), None)
    return jax.shard_map(local_block, mesh=mesh, in_specs=(row_spec, P(None), P(None, "tp", None), P("tp", None, None), P(None, "tp"), P("tp", None)), out_specs=row_spec, check_vma=False)
```

time: 382 us -> 141 us (0.37)
  waiting for transfers between devices: 173 us -> 0 us
  matrix products: 142 us -> 0 us
  Pallas kernels: 0 us -> 137 us
  other arithmetic: 50.8 us -> 0 us
  between operations: 13.5 us -> 0.01 us
    pallas_call x0 -> x1, Pallas kernels: none -> 137 us  [local_block(): pl.pallas_call(functools.partial(block_kernel, head_dim, head_rows), out_...]
    dot_general x6 -> x0, matrix products: 134 us -> none  [the longest x2 51.1 us: one_block(): jnp.einsum('qhe,khe->hqk', query_blk, key_rows, preferred_element_type=jn...]
    reduce_scatter x1 -> x0, waiting for transfers between devices: 117 us -> none  [local_block(): reduced = lax.psum_scatter(part_sum, 'tp', scatter_dimension=0, tiled=True)]
    all_gather x1 -> x0, waiting for transfers between devices: 55.9 us -> none  [local_block(): gathered = lax.all_gather(normed, 'tp', axis=0, tiled=True)]
    reduce_sum x4 -> x0, other arithmetic: 45.9 us -> none  [the longest x2 42.5 us: one_block(): exp_sum = jnp.sum(exp_scores, axis=-1, keepdims=True)]
    unnamed x1 -> x0, matrix products: 7.32 us -> none
    convert_element_type x3 -> x0, other arithmetic: 4.82 us -> none  [the longest x1 2.88 us: local_block(): return (residual + reduced).astype(jnp.bfloat16)]
  transfers between devices with their start and end apart: 2 -> 0, of which waited for: 2 -> 0; matrix products, arithmetic and copies ran while one was open for 0% -> 0% of each run, Pallas kernels for 0% -> 0%
where the time goes in v2:
time: 141 us; the launch traced here: 140 us
  Pallas kernels  137 us (97%)
  local copies, waits for them, and re-layouts  3.67 us (3%)
    pallas_call x1, Pallas kernels, local_block(): pl.pallas_call(functools.partial(block_kernel, head_dim, head_rows), out_...  137 us

profile of v2, /device:TPU:0, one launch (start us, length us, event | category | flops | bytes accessed | tf_op | source)
XLA Modules:
  0.0 140.4 jit_solution(14398595675660172803)
XLA Ops:
  0.0 1.3 reshape.3.gamma_ref
  1.3 136.7 %parallel_block.1 = bf16[512,1152]{1,0:T(8,128)(2,1)} custom-call(bf16[512,1152]{1,0:T(8,128)(2,1)} %x_hbm.1, f32[1,1152]{1,0:T(1,128)} %reshape.3.gamma_ref, bf16[2,216,1152]{2,1,0:T(8,128)(2,1)} %bitcast.3, bf16[2,72,1152]{2,1,0:T(8,128)(2,1)} %wout_hbm.1, bf16[576,1152]{1,0:T(8,128)(2,1)} %bitcast.2, bf16[576,1152]{1,0:T(8,128)(2,1)} %w2_hbm.1), custom_call_target="tpu_custom_call" | custom-call | tf_op jit(solution)/shard_map/parallel_block/pallas_call | solution.py:288
  138.0 2.4 %copy.8 = bf16[512,1152]{1,0:T(8,128)(2,1)} copy(bf16[512,1152]{1,0:T(8,128)(2,1)} %parallel_block.1) | data formatting | bytes 2359296

commit v3 on v2

--- a/solution.py
+++ b/solution.py
@@ -13,6 +13,8 @@
 UNITS = 8
 CHUNKS = 2 * UNITS
 HEADS = 4
+SUBS = 4
+SUB_ROWS = ROWS // SUBS
 F32 = jnp.float32
 BF16 = jnp.bfloat16
 ROW_MAJOR = (((1,), (0,)), ((), ()))
@@ -45,13 +47,20 @@
         return pltpu.make_async_remote_copy(src_ref=src, dst_ref=dst, send_sem=send, recv_sem=rcv,
                                             device_id={"tp": dev}, device_id_type=mesh_id)
 
+    loads = [pltpu.make_async_copy(x_hbm.at[pl.ds(half * ROWS, ROWS)], xg.at[half], load_sem.at[half]) for half in (0, 1)]
+    for cp in loads:
+        cp.start()
+    barrier = pltpu.get_barrier_semaphore()
+
+    def greet(dev):
+        pl.semaphore_signal(barrier, inc=1, device_id={"tp": dev}, device_id_type=mesh_id)
+
+    greet(x_nbr)
+    greet(y_nbr)
     wqv[:, :, head_rows - 16:, :] = jnp.zeros((2, HEADS, 16, wqv.shape[3]), BF16)
     wk[:, LANES - 64:, :] = jnp.zeros((HEADS, 64, wk.shape[2]), BF16)
     wout[:, head_rows - 16:, :] = jnp.zeros((HEADS, 16, wout.shape[2]), BF16)
-
-    barrier = pltpu.get_barrier_semaphore()
-    for dev in (sib, x_nbr, y_nbr):
-        pl.semaphore_signal(barrier, inc=1, device_id={"tp": dev}, device_id_type=mesh_id)
+    greet(sib)
 
     pairs = []
     for hh in (0, 1):
@@ -64,29 +73,27 @@
             (wout_hbm.at[hh], wout.at[h, real]),
         ]
     pairs += [(w1_hbm, w1.at[core]), (w2_hbm, w2.at[core])]
-    loads = [pltpu.make_async_copy(x_hbm.at[pl.ds(half * ROWS, ROWS)], xg.at[half], load_sem.at[half]) for half in (0, 1)]
-    loads += [pltpu.make_async_copy(src, dst, load_sem.at[2 + n]) for n, (src, dst) in enumerate(pairs)]
+
+    pl.semaphore_wait(barrier, 3)
     for cp in loads:
-        cp.start()
-
-    pl.semaphore_wait(barrier, 3)
+        cp.wait()
 
     def gather_copy(src, dst, idx, dev):
         return remote(src, xg.at[dst], gsend.at[idx], grecv.at[idx], dev)
 
-    half_1, half_2 = x_hbm.at[pl.ds(0, ROWS)], x_hbm.at[pl.ds(ROWS, ROWS)]
     g_copies = [
-        gather_copy(half_1, 2, 0, y_nbr),
-        gather_copy(half_2, 3, 1, x_nbr),
-        gather_copy(half_1, 4, 2, x_nbr),
-        gather_copy(half_2, 5, 3, y_nbr),
+        gather_copy(xg.at[0], 2, 0, y_nbr),
+        gather_copy(xg.at[1], 3, 1, x_nbr),
+        gather_copy(xg.at[0], 4, 2, x_nbr),
+        gather_copy(xg.at[1], 5, 3, y_nbr),
         gather_copy(xg.at[2], 6, 4, x_nbr),
         gather_copy(xg.at[3], 7, 5, y_nbr),
     ]
     for cp in g_copies[:4]:
         cp.start()
     w_copies = [remote(src, dst, wsend.at[n], wrecv.at[n], sib) for n, (src, dst) in enumerate(pairs)]
-    for cp in w_copies:
+    w_loads = [pltpu.make_async_copy(src, dst, load_sem.at[2 + n]) for n, (src, dst) in enumerate(pairs)]
+    for cp in w_copies + w_loads:
         cp.start()
 
     zero_rows = LANES - head_rows
@@ -108,7 +115,7 @@
         mean = jnp.mean(rows, axis=-1, keepdims=True)
         cent = rows - mean
         var = jnp.mean(cent * cent, axis=-1, keepdims=True)
-        normed = (cent * lax.rsqrt(var + LN_EPS) * gamma_ref[...]).astype(BF16)
+        normed = (cent * lax.rsqrt(var + LN_EPS) * gamma_ref[...][None, :]).astype(BF16)
         xn[unit] = normed
         keys = dot(normed, wk[...].reshape(HEADS * LANES, -1), BY_ROWS)
         qv = dot(wqv[...].reshape(2 * HEADS * head_rows, -1), normed, BY_ROWS).astype(BF16)
@@ -137,6 +144,8 @@
 
     exp_scale = (head_dim ** -0.5) * math.log2(math.e)
     groups = ROWS // 8
+    early = [c for c in range(CHUNKS) if c % UNITS < 6]
+    late = [c for c in range(CHUNKS) if c % UNITS >= 6]
 
     def score_chunk(n, c, h, q, s_ref):
         s = dot(k_all[c, h], q)
@@ -189,6 +198,32 @@
         l_st[i, h] = jnp.broadcast_to(total, l_st.shape[2:])
         acc_st[i, h] = acc
 
+    def late_span(n, h):
+        return pl.ds((h * len(late) + n) * ROWS, ROWS)
+
+    def late_scores(unit, chunks, start, s_ref):
+        for h in range(HEADS):
+            q = q_all[unit, h]
+            for n, c in enumerate(chunks):
+                s_ref[late_span(start + n, h), :] = dot(k_all[c, h], q)
+
+    def late_finish(i, s_ref):
+        for h in range(HEADS):
+            m = None
+            for n in range(len(late)):
+                mc = jnp.max(s_ref[late_span(n, h), :].reshape(groups, 8, ROWS), axis=0)
+                m = mc if m is None else jnp.maximum(m, mc)
+            m = jnp.max(m, axis=0, keepdims=True)
+            total = None
+            acc = None
+            for n, c in enumerate(late):
+                e = jnp.exp2((s_ref[late_span(n, h), :] - m) * exp_scale)
+                tc = jnp.sum(e.reshape(groups, 8, ROWS), axis=0)
+                total = tc if total is None else total + tc
+                pv = dot(v_all[c, h], e.astype(BF16))
+                acc = pv if acc is None else acc + pv
+            emit_merged(i, h, m, jnp.sum(total, axis=0, keepdims=True), acc)
+
     def emit_merged(i, h, m, total, acc):
         m_old = m_st[i, h][:1]
         top = jnp.maximum(m, m_old)
@@ -206,21 +241,22 @@
     def reduce_copy(idx, src, dev):
         return remote(part.at[src], recv.at[idx], rsend.at[idx], rrecv.at[idx], dev)
 
-    r_copies = [
-        reduce_copy(0, 2, y_nbr),
-        reduce_copy(1, 3, x_nbr),
-        reduce_copy(2, 6, y_nbr),
-        reduce_copy(3, 7, x_nbr),
-        reduce_copy(4, 4, x_nbr),
-        reduce_copy(5, 5, y_nbr),
-    ]
-
-    for cp in loads[2:]:
+    def sub_copies(idx, src, dev):
+        copies = []
+        for sub in range(SUBS):
+            span = pl.ds(sub * SUB_ROWS, SUB_ROWS)
+            sem = 2 + (idx - 2) * SUBS + sub
+            copies.append(remote(part.at[src, span], recv.at[idx, span], rsend.at[sem], rrecv.at[sem], dev))
+        return copies
+
+    r_first = [reduce_copy(0, 2, y_nbr), reduce_copy(1, 3, x_nbr)]
+    r_join = [sub_copies(2, 6, y_nbr), sub_copies(3, 7, x_nbr)]
+    r_last = [sub_copies(4, 4, x_nbr), sub_copies(5, 5, y_nbr)]
+
+    for cp in w_loads:
         cp.wait()
     for cp in w_copies:
         cp.wait_recv()
-    for cp in loads[:2]:
-        cp.wait()
     lax.fori_loop(0, 2, project, 0)
     lax.fori_loop(0, 2, mlp, 0)
     g_copies[0].wait_recv()
@@ -233,47 +269,59 @@
     g_copies[3].wait_recv()
     lax.fori_loop(4, 6, project, 0)
     lax.fori_loop(0, 6, kv_wait, 0)
-    early = [c for c in range(CHUNKS) if c % UNITS < 6]
-    late = [c for c in range(CHUNKS) if c % UNITS >= 6]
     attend(2, lambda i: 2 + i, early, emit_state, lambda i, unit: None)
     g_copies[4].wait_recv()
     g_copies[5].wait_recv()
     lax.fori_loop(6, 8, project, 0)
+    late_own = late[:len(late) // 2]
+    late_sib = late[len(late) // 2:]
+    late_scores(2, late_own, 0, s_even)
+    late_scores(3, late_own, 0, s_odd)
     lax.fori_loop(6, 8, kv_wait, 0)
-
-    def after_first(i, unit):
+    late_scores(2, late_sib, len(late_own), s_even)
+    late_scores(3, late_sib, len(late_own), s_odd)
+    late_finish(0, s_even)
+    add_heads(2)
+    r_first[0].start()
+    late_finish(1, s_odd)
+    add_heads(3)
+    r_first[1].start()
+    lax.fori_loop(4, 8, mlp, 0)
+
+    def later_unit(i):
+        p = i // 2
+        return 2 * (3 - p - p // 2) + lax.rem(i, 2)
+
+    def after_later(i, unit):
         add_heads(unit)
         for step in (0, 1):
             @pl.when(i == step)
             def _():
-                r_copies[step].start()
-
-    attend(2, lambda i: 2 + i, late, emit_merged, after_first)
-    lax.fori_loop(4, 8, mlp, 0)
-
-    def later_unit(i):
-        p = i // 2
-        return 2 * (3 - p - p // 2) + lax.rem(i, 2)
-
-    def after_later(i, unit):
-        add_heads(unit)
-        for step in range(4):
-            @pl.when(i == step)
-            def _():
-                if step >= 2:
-                    r_copies[step].wait_recv()
-                    part[step + 2] += recv[step]
-                r_copies[step + 2].start()
+                for cp in r_join[step]:
+                    cp.start()
 
     attend(6, later_unit, list(range(CHUNKS)), emit_out, after_later)
 
-    for half, first, second in ((0, 0, 4), (1, 1, 5)):
-        r_copies[first].wait_recv()
-        r_copies[second].wait_recv()
-        span = pl.ds(half * ROWS, ROWS)
-        y_ref[span, :] = (xg[half].astype(F32) + part[half] + recv[first] + recv[second]).astype(BF16)
-    for cp in g_copies + w_copies + r_copies:
+    for sub in range(SUBS):
+        span = pl.ds(sub * SUB_ROWS, SUB_ROWS)
+        for n in (0, 1):
+            r_join[n][sub].wait_recv()
+            part[4 + n, span, :] += recv[2 + n, span, :]
+            r_last[n][sub].start()
+    for cp in r_first:
+        cp.wait_recv()
+    for half in (0, 1):
+        part[half] += xg[half].astype(F32) + recv[half]
+    for sub in range(SUBS):
+        span = pl.ds(sub * SUB_ROWS, SUB_ROWS)
+        for half in (0, 1):
+            r_last[half][sub].wait_recv()
+            y_ref[pl.ds(half * ROWS + sub * SUB_ROWS, SUB_ROWS), :] = (part[half, span, :] + recv[4 + half, span, :]).astype(BF16)
+    for cp in g_copies + w_copies + r_first:
         cp.wait_send()
+    for group in r_join + r_last:
+        for cp in group:
+            cp.wait_send()
 
 
 def solution(mesh):
@@ -287,7 +335,7 @@
         dma = pltpu.SemaphoreType.DMA
         return pl.pallas_call(
             functools.partial(block_kernel, head_dim, head_rows),
-            out_shape=jax.ShapeDtypeStruct(x_loc.shape, BF16),
+            out_shape=pltpu.VMEM(x_loc.shape, BF16),
             in_specs=[hbm, vmem, hbm, hbm, hbm, hbm],
             out_specs=vmem,
             scratch_shapes=[
@@ -312,11 +360,11 @@
                 pltpu.VMEM((2, HEADS, 8, ROWS), F32),
                 pltpu.VMEM((2, HEADS, 8, ROWS), F32),
                 dma((12,)), dma((10,)), dma((10,)), dma((6,)), dma((6,)),
-                dma((2, UNITS)), dma((2, UNITS)), dma((6,)), dma((6,)),
+                dma((2, UNITS)), dma((2, UNITS)), dma((2 + 4 * SUBS,)), dma((2 + 4 * SUBS,)),
             ],
-            compiler_params=pltpu.CompilerParams(collective_id=0, has_side_effects=True, vmem_limit_bytes=67043328),
+            compiler_params=pltpu.CompilerParams(collective_id=0, has_side_effects=True, vmem_limit_bytes=64000000),
             name="parallel_block",
-        )(x_loc, ln_gamma.reshape(1, model_dim), w_qkv.transpose(1, 2, 0), w_out, w_up.T, w_down)
+        )(x_loc, ln_gamma, w_qkv.transpose(1, 2, 0), w_out, w_up.T, w_down)
 
     row_spec = P(("data", "tp"), None)
     return jax.shard_map(local_block, mesh=mesh, in_specs=(row_spec, P(None), P(None, "tp", None), P("tp", None, None), P(None, "tp"), P("tp", None)), out_specs=row_spec, check_vma=False)

time: 141 us -> 132 us (0.936)
  Pallas kernels: 137 us -> 131 us
  local copies, waits for them, and re-layouts: 3.67 us -> 1.02 us
    pallas_call x1, Pallas kernels: 137 us -> 131 us  [local_block(): pl.pallas_call(functools.partial(block_kernel, head_dim, head_rows), out_...]
where the time goes in v3:
time: 132 us
  Pallas kernels  131 us (99%)
    pallas_call x1, Pallas kernels, local_block(): pl.pallas_call(functools.partial(block_kernel, head_dim, head_rows), out_...  131 us

profile of v3, /device:TPU:0, one launch (start us, length us, event | category | flops | bytes accessed | tf_op | source)
XLA Modules:
  0.0 131.8 jit_solution(8397591227921339271)
XLA Ops:
  0.0 130.8 %parallel_block.1 = bf16[512,1152]{1,0:T(8,128)(2,1)S(1)} custom-call(bf16[512,1152]{1,0:T(8,128)(2,1)} %x_hbm.1, f32[1152]{0:T(1024)} %gamma_ref.1, bf16[2,216,1152]{2,1,0:T(8,128)(2,1)} %bitcast.3, bf16[2,72,1152]{2,1,0:T(8,128)(2,1)} %wout_hbm.1, bf16[576,1152]{1,0:T(8,128)(2,1)} %bitcast.2, bf16[576,1152]{1,0:T(8,128)(2,1)} %w2_hbm.1), custom_call_target="tpu_custom_call" | custom-call | tf_op jit(solution)/shard_map/parallel_block/pallas_call | solution.py:336
  130.8 1.0 copy.8

commit v4 on v3

--- a/solution.py
+++ b/solution.py
@@ -13,8 +13,8 @@
 UNITS = 8
 CHUNKS = 2 * UNITS
 HEADS = 4
-SUBS = 4
-SUB_ROWS = ROWS // SUBS
+HALF = ROWS // 2
+QUARTER = ROWS // 4
 F32 = jnp.float32
 BF16 = jnp.bfloat16
 ROW_MAJOR = (((1,), (0,)), ((), ()))
@@ -32,7 +32,7 @@
 
 def block_kernel(head_dim, head_rows, x_hbm, gamma_ref, wqkv_hbm, wout_hbm, w1_hbm, w2_hbm, y_ref,
                  xg, xn, wqv, wk, wout, w1, w2, q_all, k_all, v_all, part, recv, s_even, s_odd, m_even, m_odd, o_t,
-                 acc_st, m_st, l_st,
+                 acc_st, m_st, l_st, m_all,
                  load_sem, wsend, wrecv, gsend, grecv, kvsend, kvrecv, rsend, rrecv):
     me = lax.axis_index("tp")
     core = lax.rem(me, 2)
@@ -78,18 +78,17 @@
     for cp in loads:
         cp.wait()
 
-    def gather_copy(src, dst, idx, dev):
-        return remote(src, xg.at[dst], gsend.at[idx], grecv.at[idx], dev)
-
-    g_copies = [
-        gather_copy(xg.at[0], 2, 0, y_nbr),
-        gather_copy(xg.at[1], 3, 1, x_nbr),
-        gather_copy(xg.at[0], 4, 2, x_nbr),
-        gather_copy(xg.at[1], 5, 3, y_nbr),
-        gather_copy(xg.at[2], 6, 4, x_nbr),
-        gather_copy(xg.at[3], 7, 5, y_nbr),
-    ]
-    for cp in g_copies[:4]:
+    top, low = pl.ds(0, HALF), pl.ds(HALF, HALF)
+    parts = (top, low)
+
+    def gather_copy(src, src_span, dst, dst_span, idx, dev):
+        return remote(xg.at[src, src_span], xg.at[dst, dst_span], gsend.at[idx], grecv.at[idx], dev)
+
+    g_first = [(gather_copy(0, parts[j], 2 + j, top, j, y_nbr), gather_copy(1, parts[j], 2 + j, low, 2 + j, x_nbr)) for j in (0, 1)]
+    g_second = [(gather_copy(0, parts[j], 4 + j, top, 4 + j, x_nbr), gather_copy(1, parts[j], 4 + j, low, 6 + j, y_nbr)) for j in (0, 1)]
+    g_diag = [(gather_copy(2 + j, top, 6 + j, top, 8 + j, x_nbr), gather_copy(2 + j, low, 6 + j, low, 10 + j, y_nbr)) for j in (0, 1)]
+    g_copies = [cp for group in (g_first, g_second, g_diag) for two in group for cp in two]
+    for cp in g_copies[:8]:
         cp.start()
     w_copies = [remote(src, dst, wsend.at[n], wrecv.at[n], sib) for n, (src, dst) in enumerate(pairs)]
     w_loads = [pltpu.make_async_copy(src, dst, load_sem.at[2 + n]) for n, (src, dst) in enumerate(pairs)]
@@ -118,14 +117,25 @@
         normed = (cent * lax.rsqrt(var + LN_EPS) * gamma_ref[...][None, :]).astype(BF16)
         xn[unit] = normed
         keys = dot(normed, wk[...].reshape(HEADS * LANES, -1), BY_ROWS)
-        qv = dot(wqv[...].reshape(2 * HEADS * head_rows, -1), normed, BY_ROWS).astype(BF16)
         for h in range(HEADS):
             k_all[unit, h] = keys[:, h * LANES:(h + 1) * LANES].astype(BF16)
-            q_all[unit, h, :head_rows] = qv[h * head_rows:(h + 1) * head_rows]
-            v_all[unit, h] = qv[(HEADS + h) * head_rows:(HEADS + h + 1) * head_rows]
-        for cp in kv_copies(unit):
-            cp.start()
-        return 0
+        k_copy, v_copy = kv_copies(unit)
+        k_copy.start()
+        values = dot(wqv[1].reshape(HEADS * head_rows, -1), normed, BY_ROWS).astype(BF16)
+        for h in range(HEADS):
+            v_all[unit, h] = values[h * head_rows:(h + 1) * head_rows]
+        v_copy.start()
+        return 0
+
+    def project_queries(unit, _):
+        queries = dot(wqv[0].reshape(HEADS * head_rows, -1), xn[unit], BY_ROWS).astype(BF16)
+        for h in range(HEADS):
+            q_all[unit, h, :head_rows] = queries[h * head_rows:(h + 1) * head_rows]
+        return 0
+
+    def project_both(unit, _):
+        project(unit, 0)
+        return project_queries(unit, 0)
 
     def mlp(unit, _):
         rows = xn[unit]
@@ -144,8 +154,10 @@
 
     exp_scale = (head_dim ** -0.5) * math.log2(math.e)
     groups = ROWS // 8
-    early = [c for c in range(CHUNKS) if c % UNITS < 6]
-    late = [c for c in range(CHUNKS) if c % UNITS >= 6]
+
+    def chunks_of(*units):
+        return list(units) + [UNITS + u for u in units]
+
 
     def score_chunk(n, c, h, q, s_ref):
         s = dot(k_all[c, h], q)
@@ -198,39 +210,38 @@
         l_st[i, h] = jnp.broadcast_to(total, l_st.shape[2:])
         acc_st[i, h] = acc
 
-    def late_span(n, h):
-        return pl.ds((h * len(late) + n) * ROWS, ROWS)
-
-    def late_scores(unit, chunks, start, s_ref):
-        for h in range(HEADS):
-            q = q_all[unit, h]
+    def more_chunks(i, chunks, emit, s_ref):
+        for h in range(HEADS):
+            q = q_all[2 + i, h]
+            m = None
             for n, c in enumerate(chunks):
-                s_ref[late_span(start + n, h), :] = dot(k_all[c, h], q)
-
-    def late_finish(i, s_ref):
-        for h in range(HEADS):
-            m = None
-            for n in range(len(late)):
-                mc = jnp.max(s_ref[late_span(n, h), :].reshape(groups, 8, ROWS), axis=0)
+                mc = score_chunk(h * len(chunks) + n, c, h, q, s_ref)
                 m = mc if m is None else jnp.maximum(m, mc)
-            m = jnp.max(m, axis=0, keepdims=True)
+            m_all[h] = m
+        for h in range(HEADS):
+            m = jnp.max(m_all[h], axis=0, keepdims=True)
             total = None
             acc = None
-            for n, c in enumerate(late):
-                e = jnp.exp2((s_ref[late_span(n, h), :] - m) * exp_scale)
+            for n, c in enumerate(chunks):
+                e = jnp.exp2((s_ref[pl.ds((h * len(chunks) + n) * ROWS, ROWS), :] - m) * exp_scale)
                 tc = jnp.sum(e.reshape(groups, 8, ROWS), axis=0)
                 total = tc if total is None else total + tc
                 pv = dot(v_all[c, h], e.astype(BF16))
                 acc = pv if acc is None else acc + pv
-            emit_merged(i, h, m, jnp.sum(total, axis=0, keepdims=True), acc)
-
-    def emit_merged(i, h, m, total, acc):
+            emit(i, h, m, jnp.sum(total, axis=0, keepdims=True), acc)
+
+    def joined(i, h, m, total, acc):
         m_old = m_st[i, h][:1]
-        top = jnp.maximum(m, m_old)
-        a_new = jnp.exp2((m - top) * exp_scale)
-        a_old = jnp.exp2((m_old - top) * exp_scale)
-        denom = total * a_new + l_st[i, h][:1] * a_old
-        o_t[h] = ((acc * a_new + acc_st[i, h] * a_old) / denom).astype(BF16)
+        high = jnp.maximum(m, m_old)
+        a_new = jnp.exp2((m - high) * exp_scale)
+        a_old = jnp.exp2((m_old - high) * exp_scale)
+        return high, total * a_new + l_st[i, h][:1] * a_old, acc * a_new + acc_st[i, h] * a_old
+
+    def emit_joined(i, h, m, total, acc):
+        emit_state(i, h, *joined(i, h, m, total, acc))
+
+    def emit_last(i, h, m, total, acc):
+        emit_out(i, h, *joined(i, h, m, total, acc))
 
     def emit_out(i, h, m, total, acc):
         o_t[h] = (acc / total).astype(BF16)
@@ -238,54 +249,64 @@
     def add_heads(unit):
         part[unit] += dot(o_t[...].reshape(HEADS * head_rows, ROWS), wout[...].reshape(HEADS * head_rows, -1), BY_COLS)
 
-    def reduce_copy(idx, src, dev):
-        return remote(part.at[src], recv.at[idx], rsend.at[idx], rrecv.at[idx], dev)
-
-    def sub_copies(idx, src, dev):
-        copies = []
-        for sub in range(SUBS):
-            span = pl.ds(sub * SUB_ROWS, SUB_ROWS)
-            sem = 2 + (idx - 2) * SUBS + sub
-            copies.append(remote(part.at[src, span], recv.at[idx, span], rsend.at[sem], rrecv.at[sem], dev))
-        return copies
-
-    r_first = [reduce_copy(0, 2, y_nbr), reduce_copy(1, 3, x_nbr)]
-    r_join = [sub_copies(2, 6, y_nbr), sub_copies(3, 7, x_nbr)]
-    r_last = [sub_copies(4, 4, x_nbr), sub_copies(5, 5, y_nbr)]
+    def reduce_copy(src, dst, start, size, sem, dev):
+        span = pl.ds(start, size)
+        return remote(part.at[src, span], recv.at[dst, span], rsend.at[sem], rrecv.at[sem], dev)
+
+    r_first = [(reduce_copy(2 + j, j, 0, HALF, 2 * j, y_nbr), reduce_copy(2 + j, j, HALF, HALF, 2 * j + 1, x_nbr)) for j in (0, 1)]
+    quarters = (0, 2, 1, 3)
+
+    def quarter_copies(src, dst, sem, first, second):
+        return [reduce_copy(src, dst, n * QUARTER, QUARTER, sem + n, first if n < 2 else second) for n in range(4)]
+
+    r_join = [quarter_copies(6 + j, 2 + j, 4 + 4 * j, y_nbr, x_nbr) for j in (0, 1)]
+    r_last = [quarter_copies(4 + j, 4 + j, 12 + 4 * j, x_nbr, y_nbr) for j in (0, 1)]
 
     for cp in w_loads:
         cp.wait()
     for cp in w_copies:
         cp.wait_recv()
-    lax.fori_loop(0, 2, project, 0)
+    lax.fori_loop(0, 2, project_both, 0)
     lax.fori_loop(0, 2, mlp, 0)
-    g_copies[0].wait_recv()
-    g_copies[4].start()
-    g_copies[1].wait_recv()
-    g_copies[5].start()
-    lax.fori_loop(2, 4, project, 0)
+    for j in (0, 1):
+        for cp, onward in zip(g_first[j], g_diag[j]):
+            cp.wait_recv()
+            onward.start()
+    lax.fori_loop(2, 4, project_both, 0)
     lax.fori_loop(2, 4, mlp, 0)
-    g_copies[2].wait_recv()
-    g_copies[3].wait_recv()
-    lax.fori_loop(4, 6, project, 0)
-    lax.fori_loop(0, 6, kv_wait, 0)
-    attend(2, lambda i: 2 + i, early, emit_state, lambda i, unit: None)
-    g_copies[4].wait_recv()
-    g_copies[5].wait_recv()
-    lax.fori_loop(6, 8, project, 0)
-    late_own = late[:len(late) // 2]
-    late_sib = late[len(late) // 2:]
-    late_scores(2, late_own, 0, s_even)
-    late_scores(3, late_own, 0, s_odd)
-    lax.fori_loop(6, 8, kv_wait, 0)
-    late_scores(2, late_sib, len(late_own), s_even)
-    late_scores(3, late_sib, len(late_own), s_odd)
-    late_finish(0, s_even)
-    add_heads(2)
-    r_first[0].start()
-    late_finish(1, s_odd)
-    add_heads(3)
-    r_first[1].start()
+    lax.fori_loop(0, 4, kv_wait, 0)
+    attend(2, lambda i: 2 + i, chunks_of(0, 1, 2, 3), emit_state, lambda i, unit: None)
+    for j in (0, 1):
+        for cp in g_second[j]:
+            cp.wait_recv()
+    lax.fori_loop(4, 6, project_both, 0)
+    lax.fori_loop(4, 6, kv_wait, 0)
+
+    def next_chunks(i, _):
+        more_chunks(i, chunks_of(4, 5), emit_joined, s_even)
+        return 0
+
+    lax.fori_loop(0, 2, next_chunks, 0)
+    for cp in g_diag[0]:
+        cp.wait_recv()
+    project_both(6, 0)
+    kv_wait(6, 0)
+
+    def diag_chunks(i, _):
+        more_chunks(i, chunks_of(6), emit_joined, s_even)
+        return 0
+
+    lax.fori_loop(0, 2, diag_chunks, 0)
+    for cp in g_diag[1]:
+        cp.wait_recv()
+    project(7, 0)
+    project_queries(7, 0)
+    kv_wait(7, 0)
+    for j in (0, 1):
+        more_chunks(j, chunks_of(7), emit_last, s_even)
+        add_heads(2 + j)
+        for cp in r_first[j]:
+            cp.start()
     lax.fori_loop(4, 8, mlp, 0)
 
     def later_unit(i):
@@ -297,29 +318,30 @@
         for step in (0, 1):
             @pl.when(i == step)
             def _():
-                for cp in r_join[step]:
-                    cp.start()
+                for n in quarters:
+                    r_join[step][n].start()
 
     attend(6, later_unit, list(range(CHUNKS)), emit_out, after_later)
 
-    for sub in range(SUBS):
-        span = pl.ds(sub * SUB_ROWS, SUB_ROWS)
-        for n in (0, 1):
-            r_join[n][sub].wait_recv()
-            part[4 + n, span, :] += recv[2 + n, span, :]
-            r_last[n][sub].start()
-    for cp in r_first:
-        cp.wait_recv()
-    for half in (0, 1):
-        part[half] += xg[half].astype(F32) + recv[half]
-    for sub in range(SUBS):
-        span = pl.ds(sub * SUB_ROWS, SUB_ROWS)
+    for j in (0, 1):
+        for n in quarters:
+            span = pl.ds(n * QUARTER, QUARTER)
+            r_join[j][n].wait_recv()
+            part[4 + j, span, :] += recv[2 + j, span, :]
+            r_last[j][n].start()
+    for j in (0, 1):
         for half in (0, 1):
-            r_last[half][sub].wait_recv()
-            y_ref[pl.ds(half * ROWS + sub * SUB_ROWS, SUB_ROWS), :] = (part[half, span, :] + recv[4 + half, span, :]).astype(BF16)
-    for cp in g_copies + w_copies + r_first:
+            r_first[j][half].wait_recv()
+            part[half, parts[j], :] += xg[half, parts[j], :].astype(F32) + recv[j, parts[half], :]
+    for j in (0, 1):
+        for n in quarters:
+            half, start = n // 2, j * HALF + (n % 2) * QUARTER
+            r_last[j][n].wait_recv()
+            total = part[half, pl.ds(start, QUARTER), :] + recv[4 + j, pl.ds(n * QUARTER, QUARTER), :]
+            y_ref[pl.ds(half * ROWS + start, QUARTER), :] = total.astype(BF16)
+    for cp in g_copies + w_copies:
         cp.wait_send()
-    for group in r_join + r_last:
+    for group in r_first + r_join + r_last:
         for cp in group:
             cp.wait_send()
 
@@ -359,8 +381,9 @@
                 pltpu.VMEM((2, HEADS, head_rows, ROWS), F32),
                 pltpu.VMEM((2, HEADS, 8, ROWS), F32),
                 pltpu.VMEM((2, HEADS, 8, ROWS), F32),
-                dma((12,)), dma((10,)), dma((10,)), dma((6,)), dma((6,)),
-                dma((2, UNITS)), dma((2, UNITS)), dma((2 + 4 * SUBS,)), dma((2 + 4 * SUBS,)),
+                pltpu.VMEM((HEADS, 8, ROWS), F32),
+                dma((12,)), dma((10,)), dma((10,)), dma((12,)), dma((12,)),
+                dma((2, UNITS)), dma((2, UNITS)), dma((20,)), dma((20,)),
             ],
             compiler_params=pltpu.CompilerParams(collective_id=0, has_side_effects=True, vmem_limit_bytes=64000000),
             name="parallel_block",

time: 132 us -> 129 us (0.977)
  Pallas kernels: 131 us -> 128 us
    pallas_call x1, Pallas kernels: 131 us -> 128 us  [local_block(): pl.pallas_call(functools.partial(block_kernel, head_dim, head_rows), out_...]
where the time goes in v4:
time: 129 us
  Pallas kernels  128 us (99%)
    pallas_call x1, Pallas kernels, local_block(): pl.pallas_call(functools.partial(block_kernel, head_dim, head_rows), out_...  128 us

profile of v4, /device:TPU:0, one launch (start us, length us, event | category | flops | bytes accessed | tf_op | source)
XLA Modules:
  0.0 128.6 jit_solution(2689554005053998276)
XLA Ops:
  0.0 127.6 %parallel_block.1 = bf16[512,1152]{1,0:T(8,128)(2,1)S(1)} custom-call(bf16[512,1152]{1,0:T(8,128)(2,1)} %x_hbm.1, f32[1152]{0:T(1024)} %gamma_ref.1, bf16[2,216,1152]{2,1,0:T(8,128)(2,1)} %bitcast.3, bf16[2,72,1152]{2,1,0:T(8,128)(2,1)} %wout_hbm.1, bf16[576,1152]{1,0:T(8,128)(2,1)} %bitcast.2, bf16[576,1152]{1,0:T(8,128)(2,1)} %w2_hbm.1), custom_call_target="tpu_custom_call" | custom-call | tf_op jit(solution)/shard_map/parallel_block/pallas_call | solution.py:358
  127.6 1.0 copy.8

commit v5 on v4

--- a/solution.py
+++ b/solution.py
@@ -86,7 +86,10 @@
 
     g_first = [(gather_copy(0, parts[j], 2 + j, top, j, y_nbr), gather_copy(1, parts[j], 2 + j, low, 2 + j, x_nbr)) for j in (0, 1)]
     g_second = [(gather_copy(0, parts[j], 4 + j, top, 4 + j, x_nbr), gather_copy(1, parts[j], 4 + j, low, 6 + j, y_nbr)) for j in (0, 1)]
-    g_diag = [(gather_copy(2 + j, top, 6 + j, top, 8 + j, x_nbr), gather_copy(2 + j, low, 6 + j, low, 10 + j, y_nbr)) for j in (0, 1)]
+    g_diag = [(gather_copy(2, top, 6, top, 8, x_nbr), gather_copy(2, low, 6, low, 9, y_nbr))]
+    for q in (0, 1):
+        q_top, q_low = pl.ds(q * QUARTER, QUARTER), pl.ds(HALF + q * QUARTER, QUARTER)
+        g_diag.append((gather_copy(3, q_top, 7, q_top, 10 + q, x_nbr), gather_copy(3, q_low, 7, q_low, 12 + q, y_nbr)))
     g_copies = [cp for group in (g_first, g_second, g_diag) for two in group for cp in two]
     for cp in g_copies[:8]:
         cp.start()
@@ -109,12 +112,39 @@
             remote(v_all.at[unit], v_all.at[UNITS + unit], kvsend.at[1, unit], kvrecv.at[1, unit], sib),
         )
 
-    def project(unit, _):
-        rows = xg[unit].astype(F32)
+    def normalize(rows):
+        rows = rows.astype(F32)
         mean = jnp.mean(rows, axis=-1, keepdims=True)
         cent = rows - mean
         var = jnp.mean(cent * cent, axis=-1, keepdims=True)
-        normed = (cent * lax.rsqrt(var + LN_EPS) * gamma_ref[...][None, :]).astype(BF16)
+        return (cent * lax.rsqrt(var + LN_EPS) * gamma_ref[...][None, :]).astype(BF16)
+
+    last = UNITS - 1
+
+    def last_copies(q):
+        span = parts[q]
+        return (
+            remote(k_all.at[last, :, span], k_all.at[UNITS + last, :, span], kvsend.at[q, last], kvrecv.at[q, last], sib),
+            remote(v_all.at[last, :, :, span], v_all.at[UNITS + last, :, :, span], kvsend.at[q, UNITS], kvrecv.at[q, UNITS], sib),
+        )
+
+    def project_last(q):
+        spans = (pl.ds(q * QUARTER, QUARTER), pl.ds(HALF + q * QUARTER, QUARTER))
+        normed = normalize(jnp.concatenate([xg[last, span] for span in spans], axis=0))
+        keys = dot(normed, wk[...].reshape(HEADS * LANES, -1), BY_ROWS)
+        for h in range(HEADS):
+            k_all[last, h, parts[q]] = keys[:, h * LANES:(h + 1) * LANES].astype(BF16)
+        k_copy, v_copy = last_copies(q)
+        k_copy.start()
+        values = dot(wqv[1].reshape(HEADS * head_rows, -1), normed, BY_ROWS).astype(BF16)
+        for h in range(HEADS):
+            v_all[last, h, :, parts[q]] = values[h * head_rows:(h + 1) * head_rows]
+        v_copy.start()
+        for n, span in enumerate(spans):
+            xn[last, span] = normed[n * QUARTER:(n + 1) * QUARTER]
+
+    def project(unit, _):
+        normed = normalize(xg[unit])
         xn[unit] = normed
         keys = dot(normed, wk[...].reshape(HEADS * LANES, -1), BY_ROWS)
         for h in range(HEADS):
@@ -206,42 +236,52 @@
         lax.fori_loop(0, count, one, 0)
 
     def emit_state(i, h, m, total, acc):
-        m_st[i, h] = jnp.broadcast_to(m, m_st.shape[2:])
-        l_st[i, h] = jnp.broadcast_to(total, l_st.shape[2:])
-        acc_st[i, h] = acc
-
-    def more_chunks(i, chunks, emit, s_ref):
-        for h in range(HEADS):
-            q = q_all[2 + i, h]
+        m_st[h] = jnp.broadcast_to(m, m_st.shape[1:])
+        l_st[h] = jnp.broadcast_to(total, l_st.shape[1:])
+        acc_st[h] = acc
+
+    def more_chunks(pieces, emit, s_ref, before_values=None):
+        size = ROWS if pieces[0][1] is None else HALF
+
+        def rows_of(h, n):
+            return pl.ds((h * len(pieces) + n) * size, size)
+
+        for h in range(HEADS):
+            q = q_all[2, h]
             m = None
-            for n, c in enumerate(chunks):
-                mc = score_chunk(h * len(chunks) + n, c, h, q, s_ref)
+            for n, (c, part_no) in enumerate(pieces):
+                s = dot(k_all[c, h] if part_no is None else k_all[c, h, parts[part_no]], q)
+                s_ref[rows_of(h, n), :] = s
+                mc = jnp.max(s.reshape(size // 8, 8, ROWS), axis=0)
                 m = mc if m is None else jnp.maximum(m, mc)
             m_all[h] = m
+        if before_values is not None:
+            before_values()
         for h in range(HEADS):
             m = jnp.max(m_all[h], axis=0, keepdims=True)
             total = None
             acc = None
-            for n, c in enumerate(chunks):
-                e = jnp.exp2((s_ref[pl.ds((h * len(chunks) + n) * ROWS, ROWS), :] - m) * exp_scale)
-                tc = jnp.sum(e.reshape(groups, 8, ROWS), axis=0)
+            for n, (c, part_no) in enumerate(pieces):
+                e = jnp.exp2((s_ref[rows_of(h, n), :] - m) * exp_scale)
+                tc = jnp.sum(e.reshape(size // 8, 8, ROWS), axis=0)
                 total = tc if total is None else total + tc
-                pv = dot(v_all[c, h], e.astype(BF16))
+                v = v_all[c, h] if part_no is None else v_all[c, h, :, parts[part_no]]
+                pv = dot(v, e.astype(BF16))
                 acc = pv if acc is None else acc + pv
-            emit(i, h, m, jnp.sum(total, axis=0, keepdims=True), acc)
-
-    def joined(i, h, m, total, acc):
-        m_old = m_st[i, h][:1]
+            emit(0, h, m, jnp.sum(total, axis=0, keepdims=True), acc)
+
+    def joined(h, m, total, acc):
+        m_old = m_st[h][:1]
         high = jnp.maximum(m, m_old)
         a_new = jnp.exp2((m - high) * exp_scale)
         a_old = jnp.exp2((m_old - high) * exp_scale)
-        return high, total * a_new + l_st[i, h][:1] * a_old, acc * a_new + acc_st[i, h] * a_old
+        return high, total * a_new + l_st[h][:1] * a_old, acc * a_new + acc_st[h] * a_old
 
     def emit_joined(i, h, m, total, acc):
-        emit_state(i, h, *joined(i, h, m, total, acc))
+        emit_state(i, h, *joined(h, m, total, acc))
 
     def emit_last(i, h, m, total, acc):
-        emit_out(i, h, *joined(i, h, m, total, acc))
+        emit_out(i, h, *joined(h, m, total, acc))
 
     def emit_out(i, h, m, total, acc):
         o_t[h] = (acc / total).astype(BF16)
@@ -269,66 +309,78 @@
     lax.fori_loop(0, 2, project_both, 0)
     lax.fori_loop(0, 2, mlp, 0)
     for j in (0, 1):
-        for cp, onward in zip(g_first[j], g_diag[j]):
-            cp.wait_recv()
-            onward.start()
+        for side in (0, 1):
+            g_first[j][side].wait_recv()
+            for two in g_diag[:1] if j == 0 else g_diag[1:]:
+                two[side].start()
     lax.fori_loop(2, 4, project_both, 0)
+    lax.fori_loop(0, 4, kv_wait, 0)
+    attend(1, lambda i: 2, chunks_of(0, 1, 2, 3), emit_state, lambda i, unit: None)
     lax.fori_loop(2, 4, mlp, 0)
-    lax.fori_loop(0, 4, kv_wait, 0)
-    attend(2, lambda i: 2 + i, chunks_of(0, 1, 2, 3), emit_state, lambda i, unit: None)
     for j in (0, 1):
         for cp in g_second[j]:
             cp.wait_recv()
     lax.fori_loop(4, 6, project_both, 0)
     lax.fori_loop(4, 6, kv_wait, 0)
-
-    def next_chunks(i, _):
-        more_chunks(i, chunks_of(4, 5), emit_joined, s_even)
-        return 0
-
-    lax.fori_loop(0, 2, next_chunks, 0)
+    more_chunks([(c, None) for c in chunks_of(4, 5)], emit_joined, s_even)
     for cp in g_diag[0]:
         cp.wait_recv()
     project_both(6, 0)
     kv_wait(6, 0)
-
-    def diag_chunks(i, _):
-        more_chunks(i, chunks_of(6), emit_joined, s_even)
-        return 0
-
-    lax.fori_loop(0, 2, diag_chunks, 0)
+    more_chunks([(c, None) for c in chunks_of(6)], emit_joined, s_odd)
     for cp in g_diag[1]:
         cp.wait_recv()
-    project(7, 0)
-    project_queries(7, 0)
-    kv_wait(7, 0)
-    for j in (0, 1):
-        more_chunks(j, chunks_of(7), emit_last, s_even)
-        add_heads(2 + j)
-        for cp in r_first[j]:
-            cp.start()
-    lax.fori_loop(4, 8, mlp, 0)
-
-    def later_unit(i):
-        p = i // 2
-        return 2 * (3 - p - p // 2) + lax.rem(i, 2)
-
-    def after_later(i, unit):
-        add_heads(unit)
-        for step in (0, 1):
-            @pl.when(i == step)
-            def _():
-                for n in quarters:
-                    r_join[step][n].start()
-
-    attend(6, later_unit, list(range(CHUNKS)), emit_out, after_later)
-
-    for j in (0, 1):
+    project_last(0)
+    more_chunks([(last, 0)], emit_joined, s_even)
+    for cp in g_diag[2]:
+        cp.wait_recv()
+    project_last(1)
+    for cp in last_copies(0):
+        cp.wait()
+    more_chunks([(last, 1), (UNITS + last, 0)], emit_joined, s_odd)
+    k_last, v_last = last_copies(1)
+    k_last.wait()
+    more_chunks([(UNITS + last, 1)], emit_last, s_even, before_values=v_last.wait)
+    add_heads(2)
+    for cp in r_first[0]:
+        cp.start()
+    project_queries(last, 0)
+
+    def join(j):
         for n in quarters:
             span = pl.ds(n * QUARTER, QUARTER)
             r_join[j][n].wait_recv()
             part[4 + j, span, :] += recv[2 + j, span, :]
             r_last[j][n].start()
+
+    def later_unit(i):
+        p = (i + 1) // 2
+        return 2 * (1 + 2 * ((p + 2) // 3) - p // 2 - 2 * (p // 3)) + lax.rem(i + 1, 2)
+
+    def after_later(i, unit):
+        @pl.when((i >= 1) & (i <= 4))
+        def _():
+            mlp(unit, 0)
+
+        add_heads(unit)
+
+        @pl.when(i == 0)
+        def _():
+            for cp in r_first[1]:
+                cp.start()
+
+        for step in (0, 1):
+            @pl.when(i == step + 1)
+            def _():
+                for n in quarters:
+                    r_join[step][n].start()
+
+        @pl.when(i == 4)
+        def _():
+            join(0)
+
+    attend(7, later_unit, list(range(CHUNKS)), emit_out, after_later)
+    join(1)
     for j in (0, 1):
         for half in (0, 1):
             r_first[j][half].wait_recv()
@@ -378,12 +430,12 @@
                 pltpu.VMEM((8, ROWS), F32),
                 pltpu.VMEM((8, ROWS), F32),
                 pltpu.VMEM((HEADS, head_rows, ROWS), BF16),
-                pltpu.VMEM((2, HEADS, head_rows, ROWS), F32),
-                pltpu.VMEM((2, HEADS, 8, ROWS), F32),
-                pltpu.VMEM((2, HEADS, 8, ROWS), F32),
+                pltpu.VMEM((HEADS, head_rows, ROWS), F32),
                 pltpu.VMEM((HEADS, 8, ROWS), F32),
-                dma((12,)), dma((10,)), dma((10,)), dma((12,)), dma((12,)),
-                dma((2, UNITS)), dma((2, UNITS)), dma((20,)), dma((20,)),
+                pltpu.VMEM((HEADS, 8, ROWS), F32),
+                pltpu.VMEM((HEADS, 8, ROWS), F32),
+                dma((12,)), dma((10,)), dma((10,)), dma((14,)), dma((14,)),
+                dma((2, UNITS + 1)), dma((2, UNITS + 1)), dma((20,)), dma((20,)),
             ],
             compiler_params=pltpu.CompilerParams(collective_id=0, has_side_effects=True, vmem_limit_bytes=64000000),
             name="parallel_block",

time: 129 us -> 128 us (level)
  no operation moved by 1% of the time
where the time goes in v5:
time: 128 us
  Pallas kernels  127 us (99%)
    pallas_call x1, Pallas kernels, local_block(): pl.pallas_call(functools.partial(block_kernel, head_dim, head_rows), out_...  127 us

profile of v5, /device:TPU:0, one launch (start us, length us, event | category | flops | bytes accessed | tf_op | source)
XLA Modules:
  0.0 127.6 jit_solution(12120534565616774316)
XLA Ops:
  0.0 126.6 %parallel_block.1 = bf16[512,1152]{1,0:T(8,128)(2,1)S(1)} custom-call(bf16[512,1152]{1,0:T(8,128)(2,1)} %x_hbm.1, f32[1152]{0:T(1024)} %gamma_ref.1, bf16[2,216,1152]{2,1,0:T(8,128)(2,1)} %bitcast.3, bf16[2,72,1152]{2,1,0:T(8,128)(2,1)} %wout_hbm.1, bf16[576,1152]{1,0:T(8,128)(2,1)} %bitcast.2, bf16[576,1152]{1,0:T(8,128)(2,1)} %w2_hbm.1), custom_call_target="tpu_custom_call" | custom-call | tf_op jit(solution)/shard_map/parallel_block/pallas_call | solution.py:410
  126.6 1.0 copy.8

commit v6 on v5

--- a/solution.py
+++ b/solution.py
@@ -75,21 +75,22 @@
     pairs += [(w1_hbm, w1.at[core]), (w2_hbm, w2.at[core])]
 
     pl.semaphore_wait(barrier, 3)
-    for cp in loads:
-        cp.wait()
 
     top, low = pl.ds(0, HALF), pl.ds(HALF, HALF)
     parts = (top, low)
 
-    def gather_copy(src, src_span, dst, dst_span, idx, dev):
-        return remote(xg.at[src, src_span], xg.at[dst, dst_span], gsend.at[idx], grecv.at[idx], dev)
-
-    g_first = [(gather_copy(0, parts[j], 2 + j, top, j, y_nbr), gather_copy(1, parts[j], 2 + j, low, 2 + j, x_nbr)) for j in (0, 1)]
-    g_second = [(gather_copy(0, parts[j], 4 + j, top, 4 + j, x_nbr), gather_copy(1, parts[j], 4 + j, low, 6 + j, y_nbr)) for j in (0, 1)]
-    g_diag = [(gather_copy(2, top, 6, top, 8, x_nbr), gather_copy(2, low, 6, low, 9, y_nbr))]
+    def diag_copy(src, dst, span, idx, dev):
+        return remote(xn.at[src, span], xn.at[dst, span], gsend.at[idx], grecv.at[idx], dev)
+
+    def own(half, j):
+        return x_hbm.at[pl.ds(half * ROWS + j * HALF, HALF)]
+
+    g_first = [(remote(own(0, j), xg.at[2 + j, top], gsend.at[j], grecv.at[j], y_nbr), remote(own(1, j), xg.at[2 + j, low], gsend.at[2 + j], grecv.at[2 + j], x_nbr)) for j in (0, 1)]
+    g_second = [(remote(own(0, j), xg.at[4 + j, top], gsend.at[4 + j], grecv.at[4 + j], x_nbr), remote(own(1, j), xg.at[4 + j, low], gsend.at[6 + j], grecv.at[6 + j], y_nbr)) for j in (0, 1)]
+    g_diag = [(diag_copy(2, 6, top, 8, x_nbr), diag_copy(2, 6, low, 9, y_nbr))]
     for q in (0, 1):
         q_top, q_low = pl.ds(q * QUARTER, QUARTER), pl.ds(HALF + q * QUARTER, QUARTER)
-        g_diag.append((gather_copy(3, q_top, 7, q_top, 10 + q, x_nbr), gather_copy(3, q_low, 7, q_low, 12 + q, y_nbr)))
+        g_diag.append((diag_copy(3, 7, q_top, 10 + q, x_nbr), diag_copy(3, 7, q_low, 12 + q, y_nbr)))
     g_copies = [cp for group in (g_first, g_second, g_diag) for two in group for cp in two]
     for cp in g_copies[:8]:
         cp.start()
@@ -130,7 +131,7 @@
 
     def project_last(q):
         spans = (pl.ds(q * QUARTER, QUARTER), pl.ds(HALF + q * QUARTER, QUARTER))
-        normed = normalize(jnp.concatenate([xg[last, span] for span in spans], axis=0))
+        normed = jnp.concatenate([xn[last, span] for span in spans], axis=0)
         keys = dot(normed, wk[...].reshape(HEADS * LANES, -1), BY_ROWS)
         for h in range(HEADS):
             k_all[last, h, parts[q]] = keys[:, h * LANES:(h + 1) * LANES].astype(BF16)
@@ -140,12 +141,13 @@
         for h in range(HEADS):
             v_all[last, h, :, parts[q]] = values[h * head_rows:(h + 1) * head_rows]
         v_copy.start()
-        for n, span in enumerate(spans):
-            xn[last, span] = normed[n * QUARTER:(n + 1) * QUARTER]
 
     def project(unit, _):
         normed = normalize(xg[unit])
         xn[unit] = normed
+        return keys_values(unit, normed)
+
+    def keys_values(unit, normed):
         keys = dot(normed, wk[...].reshape(HEADS * LANES, -1), BY_ROWS)
         for h in range(HEADS):
             k_all[unit, h] = keys[:, h * LANES:(h + 1) * LANES].astype(BF16)
@@ -302,18 +304,19 @@
     r_join = [quarter_copies(6 + j, 2 + j, 4 + 4 * j, y_nbr, x_nbr) for j in (0, 1)]
     r_last = [quarter_copies(4 + j, 4 + j, 12 + 4 * j, x_nbr, y_nbr) for j in (0, 1)]
 
-    for cp in w_loads:
+    for cp in loads + w_loads:
         cp.wait()
     for cp in w_copies:
         cp.wait_recv()
     lax.fori_loop(0, 2, project_both, 0)
     lax.fori_loop(0, 2, mlp, 0)
     for j in (0, 1):
-        for side in (0, 1):
-            g_first[j][side].wait_recv()
-            for two in g_diag[:1] if j == 0 else g_diag[1:]:
-                two[side].start()
-    lax.fori_loop(2, 4, project_both, 0)
+        for cp in g_first[j]:
+            cp.wait_recv()
+        project_both(2 + j, 0)
+        for two in g_diag[:1] if j == 0 else g_diag[1:]:
+            for cp in two:
+                cp.start()
     lax.fori_loop(0, 4, kv_wait, 0)
     attend(1, lambda i: 2, chunks_of(0, 1, 2, 3), emit_state, lambda i, unit: None)
     lax.fori_loop(2, 4, mlp, 0)
@@ -325,7 +328,8 @@
     more_chunks([(c, None) for c in chunks_of(4, 5)], emit_joined, s_even)
     for cp in g_diag[0]:
         cp.wait_recv()
-    project_both(6, 0)
+    keys_values(6, xn[6])
+    project_queries(6, 0)
     kv_wait(6, 0)
     more_chunks([(c, None) for c in chunks_of(6)], emit_joined, s_odd)
     for cp in g_diag[1]:
@@ -413,7 +417,7 @@
             in_specs=[hbm, vmem, hbm, hbm, hbm, hbm],
             out_specs=vmem,
             scratch_shapes=[
-                pltpu.VMEM((UNITS, ROWS, model_dim), BF16),
+                pltpu.VMEM((UNITS - 2, ROWS, model_dim), BF16),
                 pltpu.VMEM((UNITS, ROWS, model_dim), BF16),
                 pltpu.VMEM((2, HEADS, head_rows, model_dim), BF16),
                 pltpu.VMEM((HEADS, LANES, model_dim), BF16),

time: 128 us -> 127 us (level)
  no operation moved by 1% of the time
where the time goes in v6:
time: 127 us
  Pallas kernels  126 us (99%)
    pallas_call x1, Pallas kernels, local_block(): pl.pallas_call(functools.partial(block_kernel, head_dim, head_rows), out_...  126 us

profile of v6, /device:TPU:0, one launch (start us, length us, event | category | flops | bytes accessed | tf_op | source)
XLA Modules:
  0.0 127.0 jit_solution(1108675116562765032)
XLA Ops:
  0.0 125.9 %parallel_block.1 = bf16[512,1152]{1,0:T(8,128)(2,1)S(1)} custom-call(bf16[512,1152]{1,0:T(8,128)(2,1)} %x_hbm.1, f32[1152]{0:T(1024)} %gamma_ref.1, bf16[2,216,1152]{2,1,0:T(8,128)(2,1)} %bitcast.3, bf16[2,72,1152]{2,1,0:T(8,128)(2,1)} %wout_hbm.1, bf16[576,1152]{1,0:T(8,128)(2,1)} %bitcast.2, bf16[576,1152]{1,0:T(8,128)(2,1)} %w2_hbm.1), custom_call_target="tpu_custom_call" | custom-call | tf_op jit(solution)/shard_map/parallel_block/pallas_call | solution.py:414
  126.0 1.0 copy.8

commit v7 on v6

--- a/solution.py
+++ b/solution.py
@@ -31,9 +31,9 @@
 
 
 def block_kernel(head_dim, head_rows, x_hbm, gamma_ref, wqkv_hbm, wout_hbm, w1_hbm, w2_hbm, y_ref,
-                 xg, xn, wqv, wk, wout, w1, w2, q_all, k_all, v_all, part, recv, s_even, s_odd, m_even, m_odd, o_t,
+                 xg, xn, wqv, wk, wk_t, wout, w1, w2, q_all, k_all, v_all, part, recv, s_even, s_odd, m_even, m_odd, o_t,
                  acc_st, m_st, l_st, m_all,
-                 load_sem, wsend, wrecv, gsend, grecv, kvsend, kvrecv, rsend, rrecv):
+                 load_sem, pad_sem, wsend, wrecv, gsend, grecv, kvsend, kvrecv, rsend, rrecv):
     me = lax.axis_index("tp")
     core = lax.rem(me, 2)
     chip_x = lax.rem(me // 2, 2)
@@ -47,20 +47,10 @@
         return pltpu.make_async_remote_copy(src_ref=src, dst_ref=dst, send_sem=send, recv_sem=rcv,
                                             device_id={"tp": dev}, device_id_type=mesh_id)
 
+    barrier = pltpu.get_barrier_semaphore()
+    for dev in (x_nbr, y_nbr, sib):
+        pl.semaphore_signal(barrier, inc=1, device_id={"tp": dev}, device_id_type=mesh_id)
     loads = [pltpu.make_async_copy(x_hbm.at[pl.ds(half * ROWS, ROWS)], xg.at[half], load_sem.at[half]) for half in (0, 1)]
-    for cp in loads:
-        cp.start()
-    barrier = pltpu.get_barrier_semaphore()
-
-    def greet(dev):
-        pl.semaphore_signal(barrier, inc=1, device_id={"tp": dev}, device_id_type=mesh_id)
-
-    greet(x_nbr)
-    greet(y_nbr)
-    wqv[:, :, head_rows - 16:, :] = jnp.zeros((2, HEADS, 16, wqv.shape[3]), BF16)
-    wk[:, LANES - 64:, :] = jnp.zeros((HEADS, 64, wk.shape[2]), BF16)
-    wout[:, head_rows - 16:, :] = jnp.zeros((HEADS, 16, wout.shape[2]), BF16)
-    greet(sib)
 
     pairs = []
     for hh in (0, 1):
@@ -92,8 +82,13 @@
         q_top, q_low = pl.ds(q * QUARTER, QUARTER), pl.ds(HALF + q * QUARTER, QUARTER)
         g_diag.append((diag_copy(3, 7, q_top, 10 + q, x_nbr), diag_copy(3, 7, q_low, 12 + q, y_nbr)))
     g_copies = [cp for group in (g_first, g_second, g_diag) for two in group for cp in two]
-    for cp in g_copies[:8]:
+    for cp in g_copies[:8] + loads:
         cp.start()
+    wqv[:, :, head_rows - 16:, :] = jnp.zeros((2, HEADS, 16, wqv.shape[3]), BF16)
+    wk[:, LANES - 64:, :] = jnp.zeros((HEADS, 64, wk.shape[2]), BF16)
+    wout[:, head_rows - 16:, :] = jnp.zeros((HEADS, 16, wout.shape[2]), BF16)
+    pl.semaphore_signal(pad_sem, inc=1, device_id={"tp": sib}, device_id_type=mesh_id)
+    pl.semaphore_wait(pad_sem, 1)
     w_copies = [remote(src, dst, wsend.at[n], wrecv.at[n], sib) for n, (src, dst) in enumerate(pairs)]
     w_loads = [pltpu.make_async_copy(src, dst, load_sem.at[2 + n]) for n, (src, dst) in enumerate(pairs)]
     for cp in w_copies + w_loads:
@@ -132,7 +127,7 @@
     def project_last(q):
         spans = (pl.ds(q * QUARTER, QUARTER), pl.ds(HALF + q * QUARTER, QUARTER))
         normed = jnp.concatenate([xn[last, span] for span in spans], axis=0)
-        keys = dot(normed, wk[...].reshape(HEADS * LANES, -1), BY_ROWS)
+        keys = dot(normed, wk_t[...])
         for h in range(HEADS):
             k_all[last, h, parts[q]] = keys[:, h * LANES:(h + 1) * LANES].astype(BF16)
         k_copy, v_copy = last_copies(q)
@@ -148,7 +143,7 @@
         return keys_values(unit, normed)
 
     def keys_values(unit, normed):
-        keys = dot(normed, wk[...].reshape(HEADS * LANES, -1), BY_ROWS)
+        keys = dot(normed, wk_t[...])
         for h in range(HEADS):
             k_all[unit, h] = keys[:, h * LANES:(h + 1) * LANES].astype(BF16)
         k_copy, v_copy = kv_copies(unit)
@@ -308,6 +303,8 @@
         cp.wait()
     for cp in w_copies:
         cp.wait_recv()
+    for h in range(HEADS):
+        wk_t[:, h * LANES:(h + 1) * LANES] = jnp.transpose(wk[h])
     lax.fori_loop(0, 2, project_both, 0)
     lax.fori_loop(0, 2, mlp, 0)
     for j in (0, 1):
@@ -421,6 +418,7 @@
                 pltpu.VMEM((UNITS, ROWS, model_dim), BF16),
                 pltpu.VMEM((2, HEADS, head_rows, model_dim), BF16),
                 pltpu.VMEM((HEADS, LANES, model_dim), BF16),
+                pltpu.VMEM((model_dim, HEADS * LANES), BF16),
                 pltpu.VMEM((HEADS, head_rows, model_dim), BF16),
                 pltpu.VMEM((2, ff, model_dim), BF16),
                 pltpu.VMEM((2, ff, model_dim), BF16),
@@ -438,7 +436,7 @@
                 pltpu.VMEM((HEADS, 8, ROWS), F32),
                 pltpu.VMEM((HEADS, 8, ROWS), F32),
                 pltpu.VMEM((HEADS, 8, ROWS), F32),
-                dma((12,)), dma((10,)), dma((10,)), dma((14,)), dma((14,)),
+                dma((12,)), pltpu.SemaphoreType.REGULAR, dma((10,)), dma((10,)), dma((14,)), dma((14,)),
                 dma((2, UNITS + 1)), dma((2, UNITS + 1)), dma((20,)), dma((20,)),
             ],
             compiler_params=pltpu.CompilerParams(collective_id=0, has_side_effects=True, vmem_limit_bytes=64000000),

time: 127 us -> 127 us (level)
  no operation moved by 1% of the time
where the time goes in v7:
time: 127 us
  Pallas kernels  126 us (99%)
    pallas_call x1, Pallas kernels, local_block(): pl.pallas_call(functools.partial(block_kernel, head_dim, head_rows), out_...  126 us

profile of v7, /device:TPU:0, one launch (start us, length us, event | category | flops | bytes accessed | tf_op | source)
XLA Modules:
  0.0 126.7 jit_solution(11668109457973526709)
XLA Ops:
  0.0 125.7 %parallel_block.1 = bf16[512,1152]{1,0:T(8,128)(2,1)S(1)} custom-call(bf16[512,1152]{1,0:T(8,128)(2,1)} %x_hbm.1, f32[1152]{0:T(1024)} %gamma_ref.1, bf16[2,216,1152]{2,1,0:T(8,128)(2,1)} %bitcast.3, bf16[2,72,1152]{2,1,0:T(8,128)(2,1)} %wout_hbm.1, bf16[576,1152]{1,0:T(8,128)(2,1)} %bitcast.2, bf16[576,1152]{1,0:T(8,128)(2,1)} %w2_hbm.1), custom_call_target="tpu_custom_call" | custom-call | tf_op jit(solution)/shard_map/parallel_block/pallas_call | solution.py:411
  125.7 1.0 copy.8

commit v8 on v7

--- a/solution.py
+++ b/solution.py
@@ -311,9 +311,14 @@
         for cp in g_first[j]:
             cp.wait_recv()
         project_both(2 + j, 0)
-        for two in g_diag[:1] if j == 0 else g_diag[1:]:
-            for cp in two:
-                cp.start()
+        for cp in g_diag[j]:
+            cp.start()
+
+    def send_last():
+        for cp in g_diag[2]:
+            cp.start()
+
+    pl.when(core == 0)(send_last)
     lax.fori_loop(0, 4, kv_wait, 0)
     attend(1, lambda i: 2, chunks_of(0, 1, 2, 3), emit_state, lambda i, unit: None)
     lax.fori_loop(2, 4, mlp, 0)
@@ -327,6 +332,7 @@
         cp.wait_recv()
     keys_values(6, xn[6])
     project_queries(6, 0)
+    pl.when(core == 1)(send_last)
     kv_wait(6, 0)
     more_chunks([(c, None) for c in chunks_of(6)], emit_joined, s_odd)
     for cp in g_diag[1]:

time: 127 us -> 126 us (level)
  no operation moved by 1% of the time
where the time goes in v8:
time: 126 us
  Pallas kernels  125 us (99%)
    pallas_call x1, Pallas kernels, local_block(): pl.pallas_call(functools.partial(block_kernel, head_dim, head_rows), out_...  125 us

profile of v8, /device:TPU:0, one launch (start us, length us, event | category | flops | bytes accessed | tf_op | source)
XLA Modules:
  0.0 126.2 jit_solution(4752463675244056036)
XLA Ops:
  0.0 125.2 %parallel_block.1 = bf16[512,1152]{1,0:T(8,128)(2,1)S(1)} custom-call(bf16[512,1152]{1,0:T(8,128)(2,1)} %x_hbm.1, f32[1152]{0:T(1024)} %gamma_ref.1, bf16[2,216,1152]{2,1,0:T(8,128)(2,1)} %bitcast.3, bf16[2,72,1152]{2,1,0:T(8,128)(2,1)} %wout_hbm.1, bf16[576,1152]{1,0:T(8,128)(2,1)} %bitcast.2, bf16[576,1152]{1,0:T(8,128)(2,1)} %w2_hbm.1), custom_call_target="tpu_custom_call" | custom-call | tf_op jit(solution)/shard_map/parallel_block/pallas_call | solution.py:417
  125.2 1.0 copy.8

commit v9 on v8

--- a/solution.py
+++ b/solution.py
@@ -358,7 +358,10 @@
             span = pl.ds(n * QUARTER, QUARTER)
             r_join[j][n].wait_recv()
             part[4 + j, span, :] += recv[2 + j, span, :]
-            r_last[j][n].start()
+            if j == 1 and n % 2 == 1:
+                pl.when(core == 0)(r_last[j][n].start)
+            else:
+                r_last[j][n].start()
 
     def later_unit(i):
         p = (i + 1) // 2
@@ -396,6 +399,8 @@
         for n in quarters:
             half, start = n // 2, j * HALF + (n % 2) * QUARTER
             r_last[j][n].wait_recv()
+            if j == 1 and n % 2 == 0:
+                pl.when(core == 1)(r_last[j][n + 1].start)
             total = part[half, pl.ds(start, QUARTER), :] + recv[4 + j, pl.ds(n * QUARTER, QUARTER), :]
             y_ref[pl.ds(half * ROWS + start, QUARTER), :] = total.astype(BF16)
     for cp in g_copies + w_copies:

time: 126 us -> 125 us (level)
    pallas_call x1, Pallas kernels: 125 us -> 124 us  [local_block(): pl.pallas_call(functools.partial(block_kernel, head_dim, head_rows), out_...]
where the time goes in v9:
time: 125 us
  Pallas kernels  124 us (99%)
    pallas_call x1, Pallas kernels, local_block(): pl.pallas_call(functools.partial(block_kernel, head_dim, head_rows), out_...  124 us

profile of v9, /device:TPU:0, one launch (start us, length us, event | category | flops | bytes accessed | tf_op | source)
XLA Modules:
  0.0 124.7 jit_solution(5418842292006645572)
XLA Ops:
  0.0 123.7 %parallel_block.1 = bf16[512,1152]{1,0:T(8,128)(2,1)S(1)} custom-call(bf16[512,1152]{1,0:T(8,128)(2,1)} %x_hbm.1, f32[1152]{0:T(1024)} %gamma_ref.1, bf16[2,216,1152]{2,1,0:T(8,128)(2,1)} %bitcast.3, bf16[2,72,1152]{2,1,0:T(8,128)(2,1)} %wout_hbm.1, bf16[576,1152]{1,0:T(8,128)(2,1)} %bitcast.2, bf16[576,1152]{1,0:T(8,128)(2,1)} %w2_hbm.1), custom_call_target="tpu_custom_call" | custom-call | tf_op jit(solution)/shard_map/parallel_block/pallas_call | solution.py:422
  123.7 1.0 copy.8
